TPU v7x, 32 devices: a whole 2x2x4 slice. The times are simulated.
32 devices in a mesh: section: 2 (over core), dp: 4 (over y, x), seq: 4 (over z).
Axes of the slice: x: 2, y: 2, z: 4, core: 2. Of those that a mesh axis runs over, the one named last changes fastest.
Arguments:
- inputs: bfloat16 [8, 1024, 768], P('dp', 'seq'), may hold values from -8 to 8
- cotangent: bfloat16 [8, 1024, 768], P('dp', 'seq'), may hold values from -6 to 6
- question_positions: int32 [8, 64], P('dp'), may hold values from 0 to 1023, as said below
- question_counts: int32 [8], P('dp'), may hold values from 32 to 64
- query_weight: bfloat16 [2, 768, 768], P('section'), may hold values from -0.21875 to 0.21875
- key_weight: bfloat16 [2, 768, 768], P('section'), may hold values from -0.21875 to 0.21875
- value_weight: bfloat16 [2, 768, 768], P('section'), may hold values from -0.21875 to 0.21875
- output_weight: bfloat16 [2, 768, 768], P('section'), may hold values from -0.875 to 0.875
- up_weight: bfloat16 [2, 768, 3072], P('section'), may hold values from -0.21875 to 0.21875
- down_weight: bfloat16 [2, 3072, 768], P('section'), may hold values from -0.109375 to 0.109375
- key_pool: float32 [2, 5, 768], P('section'), may hold values from -2.5 to 2.5
- value_pool: float32 [2, 5, 768], P('section'), may hold values from -2.5 to 2.5
- attn_norm_gain: float32 [2, 768], P('section'), may hold values from 0.5 to 1.5
- attn_norm_bias: float32 [2, 768], P('section'), may hold values from -3 to 3
- ffn_norm_gain: float32 [2, 768], P('section'), may hold values from 0.5 to 1.5
- ffn_norm_bias: float32 [2, 768], P('section'), may hold values from -3 to 3
Outputs:
- section_outputs: bfloat16 [2, 8, 1024, 768], P('section', 'dp', 'seq')
- input_grads: bfloat16 [2, 8, 1024, 768], P('section', 'dp', 'seq')
- query_weight_grad: float32 [2, 768, 768], P('section')
- key_weight_grad: float32 [2, 768, 768], P('section')
- value_weight_grad: float32 [2, 768, 768], P('section')
- output_weight_grad: float32 [2, 768, 768], P('section')
- up_weight_grad: float32 [2, 768, 3072], P('section')
- down_weight_grad: float32 [2, 3072, 768], P('section')
- key_pool_grad: float32 [2, 5, 768], P('section')
- value_pool_grad: float32 [2, 5, 768], P('section')
- attn_norm_gain_grad: float32 [2, 768], P('section')
- attn_norm_bias_grad: float32 [2, 768], P('section')
- ffn_norm_gain_grad: float32 [2, 768], P('section')
- ffn_norm_bias_grad: float32 [2, 768], P('section')
Inputs may be any that keep to these rules, and one draw needn't show every extreme that they name: `question_positions`: each item's slots hold consecutive positions, slot c at a per-item start plus c.
All inputs are finite; a program needn't handle non-finite values.
Results may differ from a plain program's by a relative error of at most 0.014.
Values may be sent and summed in bfloat16 or wider, within the bound.
A program may use at most 320 MiB of HBM per device.

v0:
```python
import math

import jax
import jax.numpy as jnp
from jax import lax
from jax.sharding import PartitionSpec as P

DH = 64
WIN = 128
PWIN = 512
STRIDE = 4
QMAX = 64


epsilon = 1e-05
highest = lax.Precision.HIGHEST
masked_score = -1e30


def padded(shard, sides, width):
    for axis, dim in sides:
        devices, length = (lax.axis_size(axis), shard.shape[dim])
        up = [(i, (i + 1) % devices) for i in range(devices - 1)]
        down = [(j, i) for i, j in up]
        last = lax.slice_in_dim(shard, length - width, length, axis=dim)
        first = lax.slice_in_dim(shard, 0, width, axis=dim)
        before = lax.ppermute(last, axis, up)
        after = lax.ppermute(first, axis, down)
        shard = jnp.concatenate([before, shard, after], axis=dim)
    return shard


def merged(shard, axis, combine):
    everything = jax.tree.map(lambda part: lax.all_gather(part, axis), shard)
    first = jax.tree.map(lambda part: part[0], everything)

    def lap(k, so_far):
        return combine(so_far, jax.tree.map(lambda part: part[k], everything))

    return lax.fori_loop(1, lax.axis_size(axis), lap, first)


def swapped(block, axis, apart):
    count = lax.axis_size(axis)
    route = []
    for low in range(count):
        high = low | 1 << apart
        if high != low and high < count:
            route += [(low, high), (high, low)]
    return lax.ppermute(block, axis, route)


def norm_rows(state, gain, shift):
    average = jnp.mean(state, axis=-1, keepdims=True)
    centred = state - average
    variance = jnp.mean(centred * centred, axis=-1, keepdims=True)
    return centred * lax.rsqrt(variance + epsilon) * gain + shift


def gelu_exact(value):
    return jax.nn.gelu(value, approximate=False)


def pool_taps(extended, taps, rows, offset):
    centre = taps.shape[0] // 2
    total = None
    for tap in range(taps.shape[0]):
        begin = offset + tap - centre
        slab = lax.slice_in_dim(extended, begin, begin + rows, axis=0)
        slab = slab.reshape(rows // STRIDE, STRIDE, slab.shape[1])[:, 0]
        term = taps[tap] * slab
        total = term if total is None else total + term
    return total


def key_mask(row_pos, raw_first, pool_first, raw_count, pool_count, length, valid):
    half = WIN // 2
    reach = PWIN // 2
    raw_pos = raw_first + jnp.arange(raw_count, dtype=jnp.int32)
    raw_valid = (raw_pos >= 0) & (raw_pos < length)
    raw_valid = (
        raw_valid[None, :]
        & (raw_pos[None, :] >= row_pos[:, None] - half)
        & (raw_pos[None, :] < row_pos[:, None] + half)
    )
    pool_index = pool_first + jnp.arange(pool_count, dtype=jnp.int32)
    pool_valid = (pool_index >= 0) & (pool_index < length // STRIDE)
    pool_valid = (
        pool_valid[None, :]
        & (STRIDE * pool_index[None, :] >= row_pos[:, None] - reach)
        & (STRIDE * pool_index[None, :] < row_pos[:, None] + reach)
    )
    question_valid = jnp.broadcast_to(valid[None, :], (row_pos.shape[0], valid.shape[0]))
    return jnp.concatenate([raw_valid, pool_valid, question_valid], axis=1)


def inner_rows(left, right):
    return lax.dot_general(
        left, right, (((0,), (0,)), ((), ())), preferred_element_type=jnp.float32
    )


def times_transposed(left, right):
    return lax.dot_general(
        left, right, (((1,), (1,)), ((), ())), preferred_element_type=jnp.float32
    )


def merge_stats(first, second):
    top = jnp.maximum(first[0], second[0])
    total = first[1] * jnp.exp(first[0] - top) + second[1] * jnp.exp(second[0] - top)
    return (top, total)


def return_rims(grads, width):
    edges = jnp.concatenate([grads[:width], grads[-width:]], axis=0)
    arrived = padded(edges.astype(jnp.bfloat16), (("seq", 0),), width).astype(edges.dtype)
    inner = grads[width:-width]
    count = inner.shape[0]
    inner = inner + jnp.pad(arrived[:width], ((0, count - width), (0, 0)))
    return inner + jnp.pad(arrived[3 * width :], ((count - width, 0), (0, 0)))


def return_pooled(grads, width):
    edges = jnp.concatenate([grads[:width], grads[-width:]], axis=0)
    arrived = padded(edges.astype(jnp.bfloat16), (("seq", 0),), width).astype(edges.dtype)
    inner = grads[width:-width]
    inner = inner + arrived[:width]
    return inner + arrived[3 * width :]


def layer_forward(state, params, positions, count):
    rows = state.shape[0]
    width = state.shape[1]
    heads = width // DH
    scale = 1.0 / math.sqrt(DH)
    half = WIN // 2
    pool_half = PWIN // (2 * STRIDE)
    base = lax.axis_index("seq") * rows
    length = lax.axis_size("seq") * rows
    normed = norm_rows(state, params["gain_one"], params["bias_one"]).astype(jnp.bfloat16)
    query = jnp.dot(normed, params["query"], preferred_element_type=jnp.float32).astype(
        jnp.bfloat16
    )
    keys = jnp.dot(normed, params["key"], preferred_element_type=jnp.float32).astype(jnp.bfloat16)
    values = jnp.dot(normed, params["value"], preferred_element_type=jnp.float32).astype(
        jnp.bfloat16
    )
    pair = jnp.concatenate([keys, values], axis=1)
    extended = padded(pair, (("seq", 0),), half)
    taps = jnp.concatenate([params["key_pool"], params["value_pool"]], axis=1)
    pooled = pool_taps(extended.astype(jnp.float32), taps, rows, half).astype(jnp.bfloat16)
    pooled_ext = padded(pooled, (("seq", 0),), pool_half)
    slots = jnp.arange(QMAX, dtype=jnp.int32)
    valid = slots < count
    row_pos = base + jnp.arange(rows, dtype=jnp.int32)
    select = (positions[:, None] == row_pos[None, :]) & valid[:, None]
    select_low = select.astype(jnp.bfloat16)
    select_float = select.astype(jnp.float32)
    triple = jnp.concatenate([query, keys, values], axis=1)
    picked = jnp.dot(select_low, triple, preferred_element_type=jnp.float32)
    picked = lax.psum(picked.astype(jnp.bfloat16), "seq")
    question_q = picked[:, :width]
    question_k = picked[:, width : 2 * width]
    question_v = picked[:, 2 * width :]
    all_keys = jnp.concatenate([extended[:, :width], pooled_ext[:, :width], question_k], axis=0)
    all_values = jnp.concatenate([extended[:, width:], pooled_ext[:, width:], question_v], axis=0)
    mask = key_mask(
        row_pos,
        base - half,
        base // STRIDE - pool_half,
        rows + 2 * half,
        rows // STRIDE + 2 * pool_half,
        length,
        valid,
    )
    query3 = query.reshape(rows, heads, DH)
    keys3 = all_keys.reshape(-1, heads, DH)
    values3 = all_values.reshape(-1, heads, DH)
    score = jnp.einsum("thd,khd->htk", query3, keys3, preferred_element_type=jnp.float32) * scale
    score = jnp.where(mask[None], score, masked_score)
    top = jnp.max(score, axis=-1, keepdims=True)
    weights = jnp.exp(score - top)
    softened = weights / jnp.sum(weights, axis=-1, keepdims=True)
    softened_low = softened.astype(jnp.bfloat16)
    local_out = jnp.einsum(
        "htk,khd->thd", softened_low, values3, preferred_element_type=jnp.float32
    ).reshape(rows, width)
    own_keys3 = keys.reshape(rows, heads, DH)
    own_values3 = values.reshape(rows, heads, DH)
    question3 = question_q.reshape(QMAX, heads, DH)
    question_score = (
        jnp.einsum("chd,thd->hct", question3, own_keys3, preferred_element_type=jnp.float32) * scale
    )
    question_top = jnp.max(question_score, axis=-1, keepdims=True)
    question_total = jnp.sum(jnp.exp(question_score - question_top), axis=-1, keepdims=True)
    global_top, global_total = merged((question_top, question_total), "seq", merge_stats)
    log_total = global_top + jnp.log(global_total)
    question_soft = jnp.exp(question_score - log_total)
    question_soft_low = question_soft.astype(jnp.bfloat16)
    numerator = jnp.einsum(
        "hct,thd->chd", question_soft_low, own_values3, preferred_element_type=jnp.float32
    )
    exact = jnp.einsum(
        "hct,thd->chd", question_soft, own_values3.astype(jnp.float32), precision=highest
    )
    numerator, exact = (
        lax.psum(numerator.astype(jnp.bfloat16), "seq").astype(jnp.float32),
        lax.psum(exact.astype(jnp.bfloat16), "seq").astype(jnp.float32),
    )
    is_question = jnp.sum(select_float, axis=0) > 0
    replaced = jnp.dot(select_float.T, numerator.reshape(QMAX, width), precision=highest)
    mixed_low = jnp.where(is_question[:, None], replaced, local_out).astype(jnp.bfloat16)
    middle = state + jnp.dot(mixed_low, params["output"], preferred_element_type=jnp.float32)
    normed_two = norm_rows(middle, params["gain_two"], params["bias_two"]).astype(jnp.bfloat16)
    hidden = jnp.dot(normed_two, params["up"], preferred_element_type=jnp.float32)
    active = gelu_exact(hidden).astype(jnp.bfloat16)
    result = middle + jnp.dot(active, params["down"], preferred_element_type=jnp.float32)
    tape = {
        "normed": normed,
        "query3": query3,
        "extended": extended,
        "taps": taps,
        "select_low": select_low,
        "select_float": select_float,
        "is_question": is_question,
        "keys3": keys3,
        "values3": values3,
        "softened": softened,
        "softened_low": softened_low,
        "question3": question3,
        "own_keys3": own_keys3,
        "own_values3": own_values3,
        "question_soft": question_soft,
        "question_soft_low": question_soft_low,
        "exact": exact,
        "mixed_low": mixed_low,
        "middle": middle,
        "normed_two": normed_two,
        "hidden": hidden,
        "active": active,
    }
    return (result, tape)


def layer_backward(state, grad_out, params, tape):
    rows = state.shape[0]
    width = state.shape[1]
    heads = width // DH
    scale = 1.0 / math.sqrt(DH)
    half = WIN // 2
    pool_half = PWIN // (2 * STRIDE)
    grads = {}
    grad_low = grad_out.astype(jnp.bfloat16)
    grads["down"] = inner_rows(tape["active"], grad_low)
    grad_active = times_transposed(grad_low, params["down"])
    _, gelu_back = jax.vjp(gelu_exact, tape["hidden"])
    grad_hidden = gelu_back(grad_active)[0].astype(jnp.bfloat16)
    grads["up"] = inner_rows(tape["normed_two"], grad_hidden)
    grad_normed_two = times_transposed(grad_hidden, params["up"])
    _, norm_back_two = jax.vjp(norm_rows, tape["middle"], params["gain_two"], params["bias_two"])
    grad_middle, grads["gain_two"], grads["bias_two"] = norm_back_two(grad_normed_two)
    grad_middle = grad_middle + grad_out
    branch_low = grad_middle.astype(jnp.bfloat16)
    grads["output"] = inner_rows(tape["mixed_low"], branch_low)
    grad_mixed = times_transposed(branch_low, params["output"]).astype(jnp.bfloat16)
    grad_question_out = jnp.dot(tape["select_low"], grad_mixed, preferred_element_type=jnp.float32)
    grad_question_out = lax.psum(grad_question_out.astype(jnp.bfloat16), "seq")
    grad_local = jnp.where(tape["is_question"][:, None], jnp.zeros_like(grad_mixed), grad_mixed)
    grad_local3 = grad_local.reshape(rows, heads, DH)
    softened = tape["softened"]
    grad_soft = jnp.einsum(
        "thd,khd->htk", grad_local3, tape["values3"], preferred_element_type=jnp.float32
    )
    delta = jnp.sum(softened * grad_soft, axis=-1, keepdims=True)
    grad_score = (softened * (grad_soft - delta)).astype(jnp.bfloat16)
    grad_query = (
        jnp.einsum(
            "htk,khd->thd", grad_score, tape["keys3"], preferred_element_type=jnp.float32
        ).reshape(rows, width)
        * scale
    )
    grad_keys_all = (
        jnp.einsum(
            "htk,thd->khd", grad_score, tape["query3"], preferred_element_type=jnp.float32
        ).reshape(-1, width)
        * scale
    )
    grad_values_all = jnp.einsum(
        "htk,thd->khd", tape["softened_low"], grad_local3, preferred_element_type=jnp.float32
    ).reshape(-1, width)
    question_grad3 = grad_question_out.reshape(QMAX, heads, DH)
    question_soft = tape["question_soft"]
    question_grad_soft = jnp.einsum(
        "chd,thd->hct", question_grad3, tape["own_values3"], preferred_element_type=jnp.float32
    )
    question_delta = jnp.sum(question_grad3.astype(jnp.float32) * tape["exact"], axis=-1).T[
        :, :, None
    ]
    question_grad_score = (question_soft * (question_grad_soft - question_delta)).astype(
        jnp.bfloat16
    )
    grad_question_q = (
        jnp.einsum(
            "hct,thd->chd",
            question_grad_score,
            tape["own_keys3"],
            preferred_element_type=jnp.float32,
        ).reshape(QMAX, width)
        * scale
    )
    grad_own_keys = (
        jnp.einsum(
            "hct,chd->thd",
            question_grad_score,
            tape["question3"],
            preferred_element_type=jnp.float32,
        ).reshape(rows, width)
        * scale
    )
    grad_own_values = jnp.einsum(
        "hct,chd->thd",
        tape["question_soft_low"],
        question_grad3,
        preferred_element_type=jnp.float32,
    ).reshape(rows, width)
    raw_count = rows + 2 * half
    pool_count = rows // STRIDE + 2 * pool_half
    grad_raw = jnp.concatenate([grad_keys_all[:raw_count], grad_values_all[:raw_count]], axis=1)
    grad_pool = jnp.concatenate(
        [
            grad_keys_all[raw_count : raw_count + pool_count],
            grad_values_all[raw_count : raw_count + pool_count],
        ],
        axis=1,
    )
    grad_question_k = grad_keys_all[raw_count + pool_count :]
    grad_question_v = grad_values_all[raw_count + pool_count :]
    sent_q, sent_k, sent_v = (
        lax.psum(grad_question_q.astype(jnp.bfloat16), "seq").astype(jnp.float32),
        lax.psum(grad_question_k.astype(jnp.bfloat16), "seq").astype(jnp.float32),
        lax.psum(grad_question_v.astype(jnp.bfloat16), "seq").astype(jnp.float32),
    )
    own_pool = return_pooled(grad_pool, pool_half)
    pool_low = own_pool.astype(jnp.bfloat16).astype(jnp.float32)

    def pool_piece(extended_values, taps_values):
        return pool_taps(extended_values, taps_values, rows, half)

    _, pool_back = jax.vjp(pool_piece, tape["extended"].astype(jnp.float32), tape["taps"])
    grad_extended, grad_taps = pool_back(pool_low)
    own_raw = return_rims(grad_raw + grad_extended, half)
    select_t = tape["select_float"].T
    own_raw = own_raw + jnp.concatenate([grad_own_keys, grad_own_values], axis=1)
    own_raw = own_raw + jnp.dot(
        select_t, jnp.concatenate([sent_k, sent_v], axis=1), precision=highest
    )
    grad_query = grad_query + jnp.dot(select_t, sent_q, precision=highest)
    query_low = grad_query.astype(jnp.bfloat16)
    key_low = own_raw[:, :width].astype(jnp.bfloat16)
    value_low = own_raw[:, width:].astype(jnp.bfloat16)
    grads["query"] = inner_rows(tape["normed"], query_low)
    grads["key"] = inner_rows(tape["normed"], key_low)
    grads["value"] = inner_rows(tape["normed"], value_low)
    grad_normed = (
        times_transposed(query_low, params["query"])
        + times_transposed(key_low, params["key"])
        + times_transposed(value_low, params["value"])
    )
    _, norm_back_one = jax.vjp(norm_rows, state, params["gain_one"], params["bias_one"])
    grad_state, grads["gain_one"], grads["bias_one"] = norm_back_one(grad_normed)
    grads["key_pool"] = grad_taps[:, :width]
    grads["value_pool"] = grad_taps[:, width:]
    return (grad_state + grad_middle, grads)


def to_partner(block):
    return swapped(block, "section", 0)


def per_device(
    inputs,
    cotangent,
    question_positions,
    question_counts,
    query_weight,
    key_weight,
    value_weight,
    output_weight,
    up_weight,
    down_weight,
    key_pool,
    value_pool,
    attn_norm_gain,
    attn_norm_bias,
    ffn_norm_gain,
    ffn_norm_bias,
):
    names = (
        "query",
        "key",
        "value",
        "output",
        "up",
        "down",
        "key_pool",
        "value_pool",
        "gain_one",
        "bias_one",
        "gain_two",
        "bias_two",
    )
    arrays = (
        query_weight,
        key_weight,
        value_weight,
        output_weight,
        up_weight,
        down_weight,
        key_pool,
        value_pool,
        attn_norm_gain,
        attn_norm_bias,
        ffn_norm_gain,
        ffn_norm_bias,
    )
    params = {name: array[0] for name, array in zip(names, arrays)}
    section = lax.axis_index("section")
    micro = inputs.shape[0]
    rows = inputs.shape[1]
    width = inputs.shape[2]
    received = jnp.zeros((rows, width), jnp.bfloat16)
    states = []
    tapes = []
    made = []
    for tick in range(micro + 1):
        slot = jnp.clip(tick - section, 0, micro - 1)
        layer_in = jnp.where(section == 0, inputs[min(tick, micro - 1)], received)
        state = layer_in.astype(jnp.float32)
        result, tape = layer_forward(
            state, params, question_positions[slot], question_counts[slot]
        )
        result_low = result.astype(jnp.bfloat16)
        states.append(state)
        tapes.append(tape)
        made.append(result_low)
        if tick < micro:
            received = to_partner(result_low)
    produced = jnp.where(section == 0, jnp.stack(made[:micro]), jnp.stack(made[1:]))
    totals = {name: jnp.zeros(params[name].shape, jnp.float32) for name in names}
    grad_in = jnp.zeros((rows, width), jnp.bfloat16)
    back = []
    for tick in range(micro + 1):
        first = tick + section >= 1
        last = tick + section <= micro
        factor = (first & last).astype(jnp.float32)
        grad_out = jnp.where(section == 1, cotangent[max(micro - 1 - tick, 0)], grad_in)
        grad_state, grads = layer_backward(
            states[micro - tick], grad_out.astype(jnp.float32), params, tapes[micro - tick]
        )
        totals = {name: totals[name] + factor * grads[name] for name in names}
        grad_state_low = grad_state.astype(jnp.bfloat16)
        back.append(grad_state_low)
        if tick < micro:
            grad_in = to_partner(grad_state_low)
    back_grads = jnp.where(
        section == 0, jnp.stack(back[1:][::-1]), jnp.stack(back[:micro][::-1])
    )
    flat = tuple((totals[name].reshape(-1, totals[name].shape[-1]) for name in names))
    summed = lax.psum(tuple(part.astype(jnp.bfloat16) for part in flat), ("dp", "seq"))
    summed = tuple(part.astype(jnp.float32) for part in summed)
    outs = tuple((part.reshape((1,) + params[name].shape) for part, name in zip(summed, names)))
    return (
        produced[None],
        back_grads[None],
        outs[0],
        outs[1],
        outs[2],
        outs[3],
        outs[4],
        outs[5],
        outs[6],
        outs[7],
        outs[8],
        outs[9],
        outs[10],
        outs[11],
    )


def solution(mesh):
    in_specs = (
        P("dp", "seq", None),
        P("dp", "seq", None),
        P("dp", None),
        P("dp"),
        P("section", None, None),
        P("section", None, None),
        P("section", None, None),
        P("section", None, None),
        P("section", None, None),
        P("section", None, None),
        P("section", None, None),
        P("section", None, None),
        P("section", None),
        P("section", None),
        P("section", None),
        P("section", None),
    )
    out_specs = (
        P("section", "dp", "seq", None),
        P("section", "dp", "seq", None),
        P("section", None, None),
        P("section", None, None),
        P("section", None, None),
        P("section", None, None),
        P("section", None, None),
        P("section", None, None),
        P("section", None, None),
        P("section", None, None),
        P("section", None),
        P("section", None),
        P("section", None),
        P("section", None),
    )
    return jax.shard_map(
        per_device, mesh=mesh, in_specs=in_specs, out_specs=out_specs, check_vma=False
    )
```

profile of v0, /device:TPU:0, one launch (start us, length us, event | category | flops | bytes accessed | tf_op | source)
XLA Modules:
  0.0 1462.9 jit_solution(10777444024431678867)
XLA Ops:
  21.0 6.3 collective-permute-start
  45.7 3.3 fusion.461
  78.3 5.2 collective-permute-start.2
  87.9 13.1 all-gather.6
  102.0 13.3 all-gather.7
  117.2 4.1 while.51
  131.6 7.9 fusion.478
  139.5 5.6 fusion.84
  146.3 11.4 all-reduce.72.cloned.1.call-done
  160.4 11.7 multiply_convert_fusion.5
  182.5 5.2 collective-permute-start.5
  225.0 5.4 collective-permute-start.7
  235.5 13.6 all-gather.8
  250.0 13.2 all-gather.9
  265.1 4.1 while.52
  282.5 8.0 fusion.481
  290.6 5.6 fusion.80
  298.1 8.3 all-reduce.76.cloned.1.call-done
  309.7 11.6 multiply_convert_fusion.4
  330.6 5.2 collective-permute-start.10
  372.4 5.7 collective-permute-start.12
  381.4 13.6 all-gather.10
  395.3 13.1 all-gather.11
  419.5 7.5 fusion.484
  427.0 5.0 fusion.76
  432.2 11.6 all-reduce.80.cloned.1.call-done
  446.0 10.8 multiply_convert_fusion.3
  456.8 4.4 add_convert_fusion.4
  461.2 5.1 multiply_reduce_fusion.5
  471.6 5.5 multiply_reduce_fusion.2
  477.2 3.9 fusion.92
  481.1 4.2 multiply_convert_fusion.2
  492.7 5.3 fusion.420
  510.5 5.6 collective-permute-start.14
  520.2 6.5 fusion.292
  528.8 34.8 %all-reduce.94.cloned.1.call-done = (bf16[64,12,64]{2,0,1:T(8,128)(2,1)}, bf16[64,12,64]{2,0,1:T(8,128)(2,1)}) async-done(((bf16[64,12,64]{2,0,1:T(8,128)(2,1)}, bf16[64,12,64]{2,0,1:T(8,128)(2,1)}), (bf16[64,12,64]{2,0,1:T(8,128)(2,1)}, bf16[64,12,64]{2,0,1:T(8,128)(2,1)})) %all-reduce.94.cloned.1.call-update) | async-done | bytes 196624 | tf_op jit(solution)/shard_map/psum | solution.py:268
  588.8 6.5 fusion.454
  597.5 5.2 collective-permute-start.16
  609.8 32.6 %all-reduce.92.cloned.1.call-done = (bf16[64,768]{0,1:T(8,128)(2,1)}, bf16[64,768]{0,1:T(8,128)(2,1)}, bf16[64,768]{0,1:T(8,128)(2,1)}) async-done(((bf16[64,768]{0,1:T(8,128)(2,1)}, bf16[64,768]{0,1:T(8,128)(2,1)}, bf16[64,768]{0,1:T(8,128)(2,1)}), (bf16[64,768]{0,1:T(8,128)(2,1)}, bf16[64,768]{0,1:T(8,128)(2,1)}, bf16[64,768]{0,1:T(8,128)(2,1)})) %all-reduce.92.cloned.1.call-update) | async-done | bytes 294928 | tf_op jit(solution)/shard_map/psum | solution.py:340
  667.2 5.5 multiply_reduce_fusion.1
  672.8 4.1 fusion.89
  676.9 4.2 multiply_convert_fusion.1
  689.0 5.3 fusion.419
  694.3 5.0 fusion.489
  713.7 5.2 collective-permute-start.19
  727.5 33.4 %all-reduce.90.cloned.1.call-done = (bf16[64,12,64]{2,0,1:T(8,128)(2,1)}, bf16[64,12,64]{2,0,1:T(8,128)(2,1)}) async-done(((bf16[64,12,64]{2,0,1:T(8,128)(2,1)}, bf16[64,12,64]{2,0,1:T(8,128)(2,1)}), (bf16[64,12,64]{2,0,1:T(8,128)(2,1)}, bf16[64,12,64]{2,0,1:T(8,128)(2,1)})) %all-reduce.90.cloned.1.call-update) | async-done | bytes 196624 | tf_op jit(solution)/shard_map/psum | solution.py:268
  796.0 6.5 fusion.452
  804.6 5.2 collective-permute-start.21
  817.9 31.5 %all-reduce.88.cloned.1.call-done = (bf16[64,768]{0,1:T(8,128)(2,1)}, bf16[64,768]{0,1:T(8,128)(2,1)}, bf16[64,768]{0,1:T(8,128)(2,1)}) async-done(((bf16[64,768]{0,1:T(8,128)(2,1)}, bf16[64,768]{0,1:T(8,128)(2,1)}, bf16[64,768]{0,1:T(8,128)(2,1)}), (bf16[64,768]{0,1:T(8,128)(2,1)}, bf16[64,768]{0,1:T(8,128)(2,1)}, bf16[64,768]{0,1:T(8,128)(2,1)})) %all-reduce.88.cloned.1.call-update) | async-done | bytes 294928 | tf_op jit(solution)/shard_map/psum | solution.py:340
  875.2 4.4 multiply_reduce_fusion
  879.6 3.9 fusion.86
  883.4 4.2 multiply_convert_fusion
  904.8 5.2 collective-permute-start.24
  914.3 10.7 fusion.36
  925.1 10.4 fusion.37
  937.3 13.6 all-reduce.86.cloned.1.call-done
  976.7 6.5 fusion.450
  985.3 5.2 collective-permute-start.26
  996.5 33.7 %all-reduce.84.cloned.1.call-done = (bf16[64,768]{0,1:T(8,128)(2,1)}, bf16[64,768]{0,1:T(8,128)(2,1)}, bf16[64,768]{0,1:T(8,128)(2,1)}) async-done(((bf16[64,768]{0,1:T(8,128)(2,1)}, bf16[64,768]{0,1:T(8,128)(2,1)}, bf16[64,768]{0,1:T(8,128)(2,1)}), (bf16[64,768]{0,1:T(8,128)(2,1)}, bf16[64,768]{0,1:T(8,128)(2,1)}, bf16[64,768]{0,1:T(8,128)(2,1)})) %all-reduce.84.cloned.1.call-update) | async-done | bytes 294928 | tf_op jit(solution)/shard_map/psum | solution.py:340
  1044.6 4.3 fusion.135
  1057.4 82.2 %all-reduce.48 = (bf16[1,5,768]{2,1,0:T(8,128)(2,1)}, bf16[1,5,768]{2,0,1:T(2,128)(2,1)}, bf16[1,768]{1,0:T(2,128)(2,1)}, bf16[1,768]{1,0:T(2,128)(2,1)}, bf16[1,768]{1,0:T(2,128)(2,1)}, /*index=5*/bf16[1,768]{1,0:T(2,128)(2,1)}) all-reduce(bf16[1,5,768]{2,1,0:T(8,128)(2,1)} %get-tuple-element.73, ...), channel_id=1, replica_groups=mesh['section'=2,'dp'=4,'seq'=4] {'dp','seq'}, use_global_device_ids=true, to_apply=%region_93.94 | all-reduce | flops 10752 | bytes 43008 | tf_op jit(solution)/shard_map/psum | solution.py:470
  1150.6 287.1 %all-reduce.82.cloned.1.call-done = (bf16[1,768,768]{2,1,0:T(8,128)(2,1)}, bf16[1,768,768]{2,1,0:T(8,128)(2,1)}, bf16[1,768,768]{2,1,0:T(8,128)(2,1)}, bf16[1,76...) async-done(((bf16[1,768,768]{2,1,0:T(8,128)(2,1)}, bf16[1,768,768]{2,1,0:T(8,128)(2,1)}, bf16[1,768,768]{2,1,0:T(8,128)(2,1)}, ...) | async-done | bytes 14155792 | tf_op jit(solution)/shard_map/psum | solution.py:470
  1446.7 5.0 reshape.1116
  1451.7 4.5 reshape.1118
  (1141 shorter events, 516.4 us)
Async XLA Ops:
  7.2 151.8 %copy-start = (bf16[1,768,768]{2,1,0:T(8,128)(2,1)S(1)}, bf16[1,768,768]{2,1,0:T(8,128)(2,1)}, u32[]{:S(2)}) copy-start(bf16[1,768,768]{2,1,0:T(8,128)(2,1)} %param.29) | copy-start | bytes 3538948
  7.2 77.4 %all-reduce.70.cloned.1.call-start = ((), (), s32[]{:S(2)}) async-start(), calls=%async_computation | async-start | bytes 589824 | tf_op jit(solution)/shard_map/psum | solution.py:162
  18.9 138.7 %all-reduce.72.cloned.1.call-start = ((), (), s32[]{:S(2)}) async-start(), calls=%async_computation.1 | async-start | bytes 393216 | tf_op jit(solution)/shard_map/psum | solution.py:208
  19.7 23.7 %collective-permute-start.1 = (bf16[64,1536]{1,0:T(8,128)(2,1)}, bf16[64,1536]{1,0:T(8,128)(2,1)S(1)}, u32[]{:S(2)}, u32[]{:S(2)}) collective-permute-start(bf16[64,1536]{1,0:T(8,128)(2,1)} %get-tuple-element.690), channel_id=1, source_target_pairs={{1,0},{2,1},{3,2},{5,4},{6,5},{7,6},{9,8},{10,9},{11,10},{13,12},{... | collective-permute-start | bytes 589832 | tf_op jit(solution)/shard_map/ppermute | solution.py:28
  21.0 23.1 %collective-permute-start = (bf16[64,1536]{1,0:T(8,128)(2,1)S(1)}, bf16[64,1536]{1,0:T(8,128)(2,1)}, u32[]{:S(2)}, u32[]{:S(2)}) collective-permute-start(bf16[64,1536]{1,0:T(8,128)(2,1)S(1)} %get-tuple-element.689), channel_id=1, source_target_pairs={{0,1},{1,2},{2,3},{4,5},{5,6},{6,7},{8,9},{9,10},{10,11},{12,13},{... | collective-permute-start | bytes 589832 | tf_op jit(solution)/shard_map/ppermute | solution.py:27
  32.7 290.4 %copy-start.44 = (bf16[256,768]{0,1:T(8,128)(2,1)}, bf16[256,768]{0,1:T(8,128)(2,1)S(1)}, u32[]{:S(2)}) copy-start(bf16[256,768]{0,1:T(8,128)(2,1)S(1)} %copy.303) | copy-start | bytes 1179652
  77.0 47.2 %collective-permute-start.3 = (bf16[64,1536]{1,0:T(8,128)(2,1)}, bf16[64,1536]{1,0:T(8,128)(2,1)}, u32[]{:S(2)}, u32[]{:S(2)}) collective-permute-start(bf16[64,1536]{1,0:T(8,128)(2,1)} %add_convert_fusion.17), channel_id=1, source_target_pairs={{1,0},{2,1},{3,2},{5,4},{6,5},{7,6},{9,8},{10,9},{11,10},{13,12},{... | collective-permute-start | bytes 589832 | tf_op jit(solution)/shard_map/ppermute | solution.py:28
  78.3 45.9 %collective-permute-start.2 = (bf16[64,1536]{1,0:T(8,128)(2,1)}, bf16[64,1536]{1,0:T(8,128)(2,1)}, u32[]{:S(2)}, u32[]{:S(2)}) collective-permute-start(bf16[64,1536]{1,0:T(8,128)(2,1)} %add_convert_fusion.17), channel_id=1, source_target_pairs={{0,1},{1,2},{2,3},{4,5},{5,6},{6,7},{8,9},{9,10},{10,11},{12,13},{... | collective-permute-start | bytes 589832 | tf_op jit(solution)/shard_map/ppermute | solution.py:27
  86.4 39.0 %copy-start.127 = (bf16[64,768]{0,1:T(8,128)(2,1)}, bf16[64,768]{0,1:T(8,128)(2,1)S(1)}, u32[]{:S(2)}) copy-start(bf16[64,768]{0,1:T(8,128)(2,1)S(1)} %copy.456) | copy-start | bytes 294916
  87.9 235.2 %copy-start.3 = (f32[12,64,256]{2,1,0:T(8,128)}, f32[12,64,256]{2,1,0:T(8,128)S(1)}, u32[]{:S(2)}) copy-start(f32[12,64,256]{2,1,0:T(8,128)S(1)} %get-tuple-element.741) | copy-start | bytes 2359300
  102.0 23.5 %copy-start.181 = (bf16[64,768]{1,0:T(8,128)(2,1)S(1)}, bf16[64,768]{1,0:T(8,128)(2,1)}, u32[]{:S(2)}) copy-start(bf16[64,768]{1,0:T(8,128)(2,1)} %get-tuple-element.711) | copy-start | bytes 294916
  123.6 107.8 %all-reduce.74.cloned.1.call-start = ((), (), s32[]{:S(2)}) async-start(), calls=%async_computation.2 | async-start | bytes 589824 | tf_op jit(solution)/shard_map/psum | solution.py:162
  173.7 1.8 collective-permute-start.4
  175.7 132.4 %copy-start.1 = (bf16[256,768]{1,0:T(8,128)(2,1)}, bf16[256,768]{1,0:T(8,128)(2,1)S(1)}, u32[]{:S(2)}) copy-start(bf16[256,768]{1,0:T(8,128)(2,1)S(1)} %get-tuple-element.649) | copy-start | bytes 1179652
  181.2 10.6 collective-permute-start.6
  182.5 9.3 collective-permute-start.5
  191.8 114.7 %all-reduce.76.cloned.1.call-start = ((), (), s32[]{:S(2)}) async-start(), calls=%async_computation.3 | async-start | bytes 393216 | tf_op jit(solution)/shard_map/psum | solution.py:208
  223.7 48.9 %collective-permute-start.8 = (bf16[64,1536]{1,0:T(8,128)(2,1)}, bf16[64,1536]{1,0:T(8,128)(2,1)}, u32[]{:S(2)}, u32[]{:S(2)}) collective-permute-start(bf16[64,1536]{1,0:T(8,128)(2,1)} %add_convert_fusion.16), channel_id=1, source_target_pairs={{1,0},{2,1},{3,2},{5,4},{6,5},{7,6},{9,8},{10,9},{11,10},{13,12},{... | collective-permute-start | bytes 589832 | tf_op jit(solution)/shard_map/ppermute | solution.py:28
  225.0 47.6 %collective-permute-start.7 = (bf16[64,1536]{1,0:T(8,128)(2,1)}, bf16[64,1536]{1,0:T(8,128)(2,1)}, u32[]{:S(2)}, u32[]{:S(2)}) collective-permute-start(bf16[64,1536]{1,0:T(8,128)(2,1)} %add_convert_fusion.16), channel_id=1, source_target_pairs={{0,1},{1,2},{2,3},{4,5},{5,6},{6,7},{8,9},{9,10},{10,11},{12,13},{... | collective-permute-start | bytes 589832 | tf_op jit(solution)/shard_map/ppermute | solution.py:27
  235.4 88.9 %copy-start.5 = (f32[12,64,256]{2,1,0:T(8,128)}, f32[12,64,256]{2,1,0:T(8,128)S(1)}, u32[]{:S(2)}) copy-start(f32[12,64,256]{2,1,0:T(8,128)S(1)} %get-tuple-element.748) | copy-start | bytes 2359300
  272.5 106.7 %all-reduce.78.cloned.1.call-start = ((), (), s32[]{:S(2)}) async-start(), calls=%async_computation.4 | async-start | bytes 589824 | tf_op jit(solution)/shard_map/psum | solution.py:162
  323.0 2.7 collective-permute-start.9
  328.3 81.8 %copy-start.48 = (bf16[256,768]{0,1:T(8,128)(2,1)}, bf16[256,768]{0,1:T(8,128)(2,1)S(1)}, u32[]{:S(2)}) copy-start(bf16[256,768]{0,1:T(8,128)(2,1)S(1)} %copy.335) | copy-start | bytes 1179652
  329.3 51.7 %copy-start.88 = (bf16[256,768]{0,1:T(8,128)(2,1)}, bf16[256,768]{0,1:T(8,128)(2,1)S(1)}, u32[]{:S(2)}) copy-start(bf16[256,768]{0,1:T(8,128)(2,1)S(1)} %copy.336) | copy-start | bytes 1179652
  329.3 9.5 collective-permute-start.11
  330.6 9.4 collective-permute-start.10
  338.6 105.3 %all-reduce.80.cloned.1.call-start = ((), (), s32[]{:S(2)}) async-start(), calls=%async_computation.5 | async-start | bytes 393216 | tf_op jit(solution)/shard_map/psum | solution.py:208
  371.1 40.3 %collective-permute-start.13 = (bf16[64,1536]{1,0:T(8,128)(2,1)}, bf16[64,1536]{1,0:T(8,128)(2,1)}, u32[]{:S(2)}, u32[]{:S(2)}) collective-permute-start(bf16[64,1536]{1,0:T(8,128)(2,1)} %add_convert_fusion.15), channel_id=1, source_target_pairs={{1,0},{2,1},{3,2},{5,4},{6,5},{7,6},{9,8},{10,9},{11,10},{13,12},{... | collective-permute-start | bytes 589832 | tf_op jit(solution)/shard_map/ppermute | solution.py:28
  372.4 39.0 %collective-permute-start.12 = (bf16[64,1536]{1,0:T(8,128)(2,1)}, bf16[64,1536]{1,0:T(8,128)(2,1)}, u32[]{:S(2)}, u32[]{:S(2)}) collective-permute-start(bf16[64,1536]{1,0:T(8,128)(2,1)} %add_convert_fusion.15), channel_id=1, source_target_pairs={{0,1},{1,2},{2,3},{4,5},{5,6},{6,7},{8,9},{9,10},{10,11},{12,13},{... | collective-permute-start | bytes 589832 | tf_op jit(solution)/shard_map/ppermute | solution.py:27
  381.0 30.4 %copy-start.129 = (bf16[64,768]{0,1:T(8,128)(2,1)}, bf16[64,768]{0,1:T(8,128)(2,1)S(1)}, u32[]{:S(2)}) copy-start(bf16[64,768]{0,1:T(8,128)(2,1)S(1)} %copy.458) | copy-start | bytes 294916
  409.9 153.8 %all-reduce.94.cloned.1.call-start = ((), (), s32[]{:S(2)}) async-start(), calls=%async_computation.12 | async-start | bytes 786432 | tf_op jit(solution)/shard_map/psum | solution.py:268
  445.7 46.3 %copy-start.10 = (f32[256,768]{1,0:T(8,128)}, f32[256,768]{1,0:T(8,128)S(1)}, u32[]{:S(2)}) copy-start(f32[256,768]{1,0:T(8,128)S(1)} %get-tuple-element.757) | copy-start | bytes 2359300
  509.2 60.3 %collective-permute-start.15 = (bf16[64,1536]{1,0:T(8,128)(2,1)}, bf16[64,1536]{1,0:T(8,128)(2,1)}, u32[]{:S(2)}, u32[]{:S(2)}) collective-permute-start(bf16[64,1536]{1,0:T(8,128)(2,1)} %get-tuple-element.696), channel_id=1, source_target_pairs={{1,0},{2,1},{3,2},{5,4},{6,5},{7,6},{9,8},{10,9},{11,10},{13,12},{... | collective-permute-start | bytes 589832 | tf_op jit(solution)/shard_map/ppermute | solution.py:28
  510.5 59.0 %collective-permute-start.14 = (bf16[64,1536]{1,0:T(8,128)(2,1)}, bf16[64,1536]{1,0:T(8,128)(2,1)}, u32[]{:S(2)}, u32[]{:S(2)}) collective-permute-start(bf16[64,1536]{1,0:T(8,128)(2,1)} %get-tuple-element.695), channel_id=1, source_target_pairs={{0,1},{1,2},{2,3},{4,5},{5,6},{6,7},{8,9},{9,10},{10,11},{12,13},{... | collective-permute-start | bytes 589832 | tf_op jit(solution)/shard_map/ppermute | solution.py:27
  526.8 40.5 %copy-start.49 = (bf16[256,768]{0,1:T(8,128)(2,1)S(1)}, bf16[256,768]{0,1:T(8,128)(2,1)}, u32[]{:S(2)}) copy-start(bf16[256,768]{0,1:T(8,128)(2,1)} %copy-done.48) | copy-start | bytes 1179652
  526.8 115.6 %all-reduce.92.cloned.1.call-start = ((), (), s32[]{:S(2)}) async-start(), calls=%async_computation.11 | async-start | bytes 1179648 | tf_op jit(solution)/shard_map/psum | solution.py:340
  528.8 39.7 %copy-start.89 = (bf16[256,768]{0,1:T(8,128)(2,1)S(1)}, bf16[256,768]{0,1:T(8,128)(2,1)}, u32[]{:S(2)}) copy-start(bf16[256,768]{0,1:T(8,128)(2,1)} %copy-done.88) | copy-start | bytes 1179652
  596.1 11.4 collective-permute-start.17
  597.5 10.0 collective-permute-start.16
  602.8 158.1 %all-reduce.90.cloned.1.call-start = ((), (), s32[]{:S(2)}) async-start(), calls=%async_computation.10 | async-start | bytes 786432 | tf_op jit(solution)/shard_map/psum | solution.py:268
  605.1 37.3 %copy-start.116 = (f32[256,768]{1,0:T(8,128)S(1)}, f32[256,768]{1,0:T(8,128)}, u32[]{:S(2)}) copy-start(f32[256,768]{1,0:T(8,128)} %copy.354) | copy-start | bytes 2359300
  607.5 36.2 %copy-start.22 = (bf16[1,768,768]{2,1,0:T(8,128)(2,1)S(1)}, bf16[1,768,768]{2,1,0:T(8,128)(2,1)}, u32[]{:S(2)}) copy-start(bf16[1,768,768]{2,1,0:T(8,128)(2,1)} %param.26) | copy-start | bytes 3538948
  652.5 4.2 collective-permute-start.18
  712.5 55.1 %collective-permute-start.20 = (bf16[64,1536]{1,0:T(8,128)(2,1)}, bf16[64,1536]{1,0:T(8,128)(2,1)}, u32[]{:S(2)}, u32[]{:S(2)}) collective-permute-start(bf16[64,1536]{1,0:T(8,128)(2,1)} %get-tuple-element.694), channel_id=1, source_target_pairs={{1,0},{2,1},{3,2},{5,4},{6,5},{7,6},{9,8},{10,9},{11,10},{13,12},{... | collective-permute-start | bytes 589832 | tf_op jit(solution)/shard_map/ppermute | solution.py:28
  713.7 53.8 %collective-permute-start.19 = (bf16[64,1536]{1,0:T(8,128)(2,1)}, bf16[64,1536]{1,0:T(8,128)(2,1)}, u32[]{:S(2)}, u32[]{:S(2)}) collective-permute-start(bf16[64,1536]{1,0:T(8,128)(2,1)} %get-tuple-element.693), channel_id=1, source_target_pairs={{0,1},{1,2},{2,3},{4,5},{5,6},{6,7},{8,9},{9,10},{10,11},{12,13},{... | collective-permute-start | bytes 589832 | tf_op jit(solution)/shard_map/ppermute | solution.py:27
  724.3 36.6 %copy-start.6 = (f32[12,64,256]{2,1,0:T(8,128)S(1)}, f32[12,64,256]{2,1,0:T(8,128)}, u32[]{:S(2)}) copy-start(f32[12,64,256]{2,1,0:T(8,128)} %copy-done.5) | copy-start | bytes 2359300
  724.3 125.1 %all-reduce.88.cloned.1.call-start = ((), (), s32[]{:S(2)}) async-start(), calls=%async_computation.9 | async-start | bytes 1179648 | tf_op jit(solution)/shard_map/psum | solution.py:340
  803.3 12.5 collective-permute-start.22
  804.6 11.2 collective-permute-start.21
  809.8 141.0 %all-reduce.86.cloned.1.call-start = ((), (), s32[]{:S(2)}) async-start(), calls=%async_computation.8 | async-start | bytes 786432 | tf_op jit(solution)/shard_map/psum | solution.py:268
  817.1 36.0 %copy-start.2 = (bf16[256,768]{1,0:T(8,128)(2,1)S(1)}, bf16[256,768]{1,0:T(8,128)(2,1)}, u32[]{:S(2)}) copy-start(bf16[256,768]{1,0:T(8,128)(2,1)} %copy-done.1) | copy-start | bytes 1179652
  861.8 4.2 collective-permute-start.23
  903.5 54.0 %collective-permute-start.25 = (bf16[64,1536]{1,0:T(8,128)(2,1)}, bf16[64,1536]{1,0:T(8,128)(2,1)}, u32[]{:S(2)}, u32[]{:S(2)}) collective-permute-start(bf16[64,1536]{1,0:T(8,128)(2,1)} %get-tuple-element.692), channel_id=1, source_target_pairs={{1,0},{2,1},{3,2},{5,4},{6,5},{7,6},{9,8},{10,9},{11,10},{13,12},{... | collective-permute-start | bytes 589832 | tf_op jit(solution)/shard_map/ppermute | solution.py:28
  904.8 52.7 %collective-permute-start.24 = (bf16[64,1536]{1,0:T(8,128)(2,1)}, bf16[64,1536]{1,0:T(8,128)(2,1)}, u32[]{:S(2)}, u32[]{:S(2)}) collective-permute-start(bf16[64,1536]{1,0:T(8,128)(2,1)} %get-tuple-element.691), channel_id=1, source_target_pairs={{0,1},{1,2},{2,3},{4,5},{5,6},{6,7},{8,9},{9,10},{10,11},{12,13},{... | collective-permute-start | bytes 589832 | tf_op jit(solution)/shard_map/ppermute | solution.py:27
  914.2 115.9 %all-reduce.84.cloned.1.call-start = ((), (), s32[]{:S(2)}) async-start(), calls=%async_computation.7 | async-start | bytes 1179648 | tf_op jit(solution)/shard_map/psum | solution.py:340
  984.0 10.3 collective-permute-start.27
  985.3 9.0 collective-permute-start.26
  990.6 447.1 %all-reduce.82.cloned.1.call-start = ((), (), s32[]{:S(2)}) async-start(), calls=%async_computation.6 | async-start | bytes 28311552 | tf_op jit(solution)/shard_map/psum | solution.py:470
  993.1 37.0 %copy-start.115 = (f32[256,768]{1,0:T(8,128)S(1)}, f32[256,768]{1,0:T(8,128)}, u32[]{:S(2)}) copy-start(f32[256,768]{1,0:T(8,128)} %copy.388) | copy-start | bytes 2359300
  993.1 37.0 %copy-start.195 = (s32[256]{0:T(256)S(1)}, s32[256]{0:T(256)}, u32[]{:S(2)}) copy-start(s32[256]{0:T(256)} %copy-done.191) | copy-start | bytes 3076
  993.1 37.0 %copy-start.250 = (s32[64]{0:T(128)S(1)}, s32[64]{0:T(128)}, u32[]{:S(2)}) copy-start(s32[64]{0:T(128)} %copy-done.249) | copy-start | bytes 772
  993.2 37.0 %copy-start.255 = (pred[64]{0:T(512)(128)(4,1)S(1)}, pred[64]{0:T(512)(128)(4,1)}, u32[]{:S(2)}) copy-start(pred[64]{0:T(512)(128)(4,1)} %copy-done.254) | copy-start | bytes 196
  1054.3 93.8 %copy-start.39 = (f32[256,768]{1,0:T(8,128)S(1)}, f32[256,768]{1,0:T(8,128)}, u32[]{:S(2)}) copy-start(f32[256,768]{1,0:T(8,128)} %copy-done.38) | copy-start | bytes 2359300
  1054.9 94.7 %copy-start.140 = (bf16[256,768]{1,0:T(8,128)(2,1)S(1)}, bf16[256,768]{1,0:T(8,128)(2,1)}, u32[]{:S(2)}) copy-start(bf16[256,768]{1,0:T(8,128)(2,1)} %copy-done.139) | copy-start | bytes 1179652
  (294 other events, 1493.4 us)
Sparse Core Ops, SparseCore 0:
  19.0 39.4 all-reduce.69
  123.8 33.8 all-reduce.71
  191.9 35.5 all-reduce.73
  272.7 33.7 all-reduce.75
  338.7 35.6 all-reduce.77
  410.0 33.8 all-reduce.79
  526.9 36.6 all-reduce.93
  602.9 39.4 all-reduce.91
  724.5 36.3 all-reduce.89
  809.9 39.4 all-reduce.87
  914.4 36.4 all-reduce.85
  990.7 39.4 all-reduce.83
  1043.5 394.1 all-reduce.81
where the time goes:
time: 1480 us; the launch traced here: 1460 us
  waiting for transfers between devices  500 us (34%)
  local copies, waits for them, and re-layouts  278 us (19%)
  matrix products  278 us (19%)
  blocking collectives  162 us (11%)
  other arithmetic  143 us (10%)
  starting transfers between devices  82.2 us (6%)
  between operations  18.7 us (1%)
    psum x1, waiting for transfers between devices, per_device(): lax.psum(tuple((part.astype(jnp.bfloat16) for part in flat)), ('dp', 'seq'))  287 us
    psum x3, waiting for transfers between devices, layer_backward(): lax.psum(grad_question_q.astype(jnp.bfloat16), 'seq').astype(jnp.float32)  97.8 us
    psum x1, blocking collectives, per_device(): lax.psum(tuple((part.astype(jnp.bfloat16) for part in flat)), ('dp', 'seq'))  82.2 us
    psum x3, waiting for transfers between devices, layer_backward(): grad_question_out = lax.psum(grad_question_out.astype(jnp.bfloat16), 'seq')  81.8 us
    all_gather x6, blocking collectives, merged(): everything = jax.tree.map(lambda part: lax.all_gather(part, axis), shard)  79.9 us
    reshape x30, local copies, waits for them, and re-layouts, pool_taps(): slab = slab.reshape(rows // STRIDE, STRIDE, slab.shape[1])[:, 0]  72.6 us
    dot_general x18, matrix products, inner_rows(): lax.dot_general(left, right, (((0,), (0,)), ((), ())), preferred_element_...  68.7 us
    ppermute x12, starting transfers between devices, padded(): before = lax.ppermute(last, axis, up)  64.8 us
  transfers between devices with their start and end apart: 41, of which 13 were waited for; matrix products, arithmetic and copies ran while one was open for 23% of the time, Pallas kernels for 0%

commit v1 on v0

v1 whole, which is shorter than its diff:
```python
import functools
import math

import jax
import jax.numpy as jnp
from jax import lax
from jax.experimental import pallas as pl
from jax.experimental.pallas import tpu as pltpu
from jax.sharding import PartitionSpec as P

DH = 64
WIN = 128
PWIN = 512
STRIDE = 4
QMAX = 64
TAIL = 16
LANES = 128

epsilon = 1e-05
masked_score = -1e30
scale = 1.0 / math.sqrt(DH)
half = WIN // 2
pool_half = PWIN // (2 * STRIDE)
low = jnp.bfloat16
full = jnp.float32
SECTION, DP, SEQ = "section", "dp", "seq"
MESH = pl.DeviceIdType.MESH


def norm_rows(state, gain, shift):
    average = jnp.mean(state, axis=-1, keepdims=True)
    centred = state - average
    variance = jnp.mean(centred * centred, axis=-1, keepdims=True)
    return centred * lax.rsqrt(variance + epsilon) * gain + shift


def gelu_parts(value):
    spread = 0.5 + 0.5 * lax.erf(value * math.sqrt(0.5))
    slope = spread + value * jnp.exp(-0.5 * value * value) * (1.0 / math.sqrt(2.0 * math.pi))
    return (value * spread).astype(low), slope.astype(low)


def mm(left, right):
    return jnp.dot(left, right, preferred_element_type=full)


def tn(left, right):
    return lax.dot_general(left, right, (((0,), (0,)), ((), ())), preferred_element_type=full)


def nt(left, right):
    return lax.dot_general(left, right, (((1,), (1,)), ((), ())), preferred_element_type=full)


def exchange_kernel(count, plan, live, reduce, n_in, n_out, *refs):
    ins, outs = refs[:n_in], refs[n_in : n_in + n_out]
    send_sem, recv_sem, keep_sem = refs[n_in + n_out : n_in + n_out + 3]
    slots = refs[n_in + n_out + 3 :]
    me = lax.axis_index(SEQ)

    def run():
        barrier = pltpu.get_barrier_semaphore()
        for step in range(1, count):
            peer = lax.rem(me + step, count)
            pl.semaphore_signal(barrier, inc=1, device_id={SEQ: peer}, device_id_type=MESH)
        pl.semaphore_wait(barrier, count - 1)
        jobs = []
        sem = 0
        for src, first, rows, shift, dst, at in plan:
            if shift is None:
                buffer = slots[dst]
                for step in range(1, count):
                    peer = lax.rem(me + step, count)
                    copy = pltpu.make_async_remote_copy(
                        src_ref=ins[src].at[pl.ds(first, rows)],
                        dst_ref=buffer.at[step - 1],
                        send_sem=send_sem.at[sem],
                        recv_sem=recv_sem.at[sem],
                        device_id={SEQ: peer},
                        device_id_type=MESH,
                    )
                    copy.start()
                    jobs.append((copy, None, None))
                    sem += 1
            else:
                target, source = me + shift, me - shift
                can_send = (target >= 0) & (target < count)
                can_take = (source >= 0) & (source < count)
                copy = pltpu.make_async_remote_copy(
                    src_ref=ins[src].at[pl.ds(first, rows)],
                    dst_ref=outs[dst].at[pl.ds(at, rows)],
                    send_sem=send_sem.at[sem],
                    recv_sem=recv_sem.at[sem],
                    device_id={SEQ: jnp.clip(target, 0, count - 1)},
                    device_id_type=MESH,
                )

                @pl.when(can_send)
                def _():
                    copy.start()

                @pl.when(jnp.logical_not(can_take))
                def _():
                    outs[dst][pl.ds(at, rows), :] = jnp.zeros((rows, outs[dst].shape[1]), outs[dst].dtype)

                jobs.append((copy, can_send, can_take))
                sem += 1
        for copy, can_send, can_take in jobs:
            if can_send is None:
                copy.wait_send()
                copy.wait_recv()
            else:
                pl.when(can_send)(copy.wait_send)
                pl.when(can_take)(copy.wait_recv)

    if live is None:
        run()
    else:
        on = lax.axis_index(SECTION) == live
        pl.when(on)(run)

        @pl.when(jnp.logical_not(on))
        def _():
            for out in outs:
                out[...] = jnp.zeros(out.shape, out.dtype)
            for buffer in slots:
                buffer[...] = jnp.zeros(buffer.shape, buffer.dtype)

    reduce(ins, outs, slots)


def exchange(ident, live, inputs, plan, out_shapes, slot_shapes, reduce):
    count = lax.axis_size(SEQ)
    copies = sum(count - 1 if item[3] is None else 1 for item in plan)
    vmem = pl.BlockSpec(memory_space=pltpu.VMEM)
    kernel = functools.partial(
        exchange_kernel, count, plan, live, reduce, len(inputs), len(out_shapes)
    )
    return pl.pallas_call(
        kernel,
        out_shape=[jax.ShapeDtypeStruct(s, t) for s, t in out_shapes],
        in_specs=[vmem] * len(inputs),
        out_specs=[vmem] * len(out_shapes),
        scratch_shapes=[
            pltpu.SemaphoreType.DMA((copies,)),
            pltpu.SemaphoreType.DMA((copies,)),
            pltpu.SemaphoreType.DMA((1,)),
        ]
        + [pltpu.VMEM((count - 1,) + s, t) for s, t in slot_shapes],
        compiler_params=pltpu.CompilerParams(collective_id=ident, has_side_effects=True),
    )(*inputs)


def slot_sum(own, slots):
    total = own.astype(full)
    for k in range(slots.shape[0]):
        total = total + slots[k].astype(full)
    return total


def gather_rows(ident, live, state, pick):
    rows, width = state.shape
    own = TAIL + rows
    right = own + rows
    quest = right + rows
    plan = (
        (1, 0, QMAX, None, 0, 0),
        (0, rows - TAIL, TAIL, 2, 0, 0),
        (0, 0, rows, -1, 0, right),
        (0, 0, rows, 1, 0, TAIL),
    )

    def reduce(ins, outs, slots):
        outs[0][pl.ds(own, rows), :] = ins[0][...]
        outs[0][pl.ds(quest, QMAX), :] = slot_sum(ins[1][...], slots[0]).astype(low)

    return exchange(
        ident,
        live,
        (state, pick),
        plan,
        (((quest + QMAX, width), low),),
        (((QMAX, width), low),),
        reduce,
    )[0]


def return_rows(ident, live, grads, rows):
    width = grads.shape[1]
    own = TAIL + rows
    right = own + rows
    quest = right + rows
    plan = (
        (0, quest, QMAX, None, 0, 0),
        (0, 0, TAIL, -2, 4, 0),
        (0, TAIL, rows, -1, 2, 0),
        (0, right, rows, 1, 3, 0),
    )

    def reduce(ins, outs, slots):
        total = ins[0][pl.ds(own, rows), :].astype(full)
        total = total + outs[2][...].astype(full) + outs[3][...].astype(full)
        outs[0][...] = total
        outs[0][pl.ds(rows - TAIL, TAIL), :] += outs[4][...].astype(full)
        outs[1][...] = slot_sum(ins[0][pl.ds(quest, QMAX), :], slots[0])

    return exchange(
        ident,
        live,
        (grads,),
        plan,
        (
            ((rows, width), full),
            ((QMAX, width), full),
            ((rows, width), low),
            ((rows, width), low),
            ((TAIL, width), low),
        ),
        (((QMAX, width), low),),
        reduce,
    )[:2]


def broadcast(count, pieces, send_sem, recv_sem):
    me = lax.axis_index(SEQ)
    copies = []
    for k, (src, slots) in enumerate(pieces):
        for step in range(1, count):
            index = k * (count - 1) + step - 1
            copies.append(
                pltpu.make_async_remote_copy(
                    src_ref=src,
                    dst_ref=slots.at[step - 1],
                    send_sem=send_sem.at[index],
                    recv_sem=recv_sem.at[index],
                    device_id={SEQ: lax.rem(me + step, count)},
                    device_id_type=MESH,
                )
            )
    return copies


def greet(count):
    me = lax.axis_index(SEQ)
    barrier = pltpu.get_barrier_semaphore()
    for step in range(1, count):
        peer = lax.rem(me + step, count)
        pl.semaphore_signal(barrier, inc=1, device_id={SEQ: peer}, device_id_type=MESH)
    pl.semaphore_wait(barrier, count - 1)


def when_live(live, action):
    if live is None:
        action()
    else:
        pl.when(lax.axis_index(SECTION) == live)(action)


def begin_all(count, live, pieces, send_sem, recv_sem):
    def start():
        greet(count)
        for copy in broadcast(count, pieces, send_sem, recv_sem):
            copy.start()

    when_live(live, start)


def finish_all(count, live, pieces, send_sem, recv_sem):
    def finish():
        for copy in broadcast(count, pieces, send_sem, recv_sem):
            copy.wait()

    when_live(live, finish)
    if live is not None:

        @pl.when(lax.axis_index(SECTION) != live)
        def _():
            for _, slots in pieces:
                slots[...] = jnp.zeros(slots.shape, slots.dtype)


def merge_questions(numerator, stats, numerators, many, answer, merged):
    tops = [stats[...]] + [many[k] for k in range(many.shape[0])]
    parts = [numerator] + [numerators.at[k] for k in range(numerators.shape[0])]
    merged[...] = jnp.zeros_like(merged)
    for p in range(numerator.shape[1] // LANES):
        top = tops[0][2 * p : 2 * p + 1]
        for t in tops[1:]:
            top = jnp.maximum(top, t[2 * p : 2 * p + 1])
        factors = [jnp.exp(t[2 * p : 2 * p + 1] - top) for t in tops]
        total = factors[0] * tops[0][2 * p + 1 : 2 * p + 2]
        for f, t in zip(factors[1:], tops[1:]):
            total = total + f * t[2 * p + 1 : 2 * p + 2]
        merged[2 * p : 2 * p + 1, :] = top + jnp.log(total)
        value = None
        for f, part in zip(factors, parts):
            weight = jnp.transpose(jnp.broadcast_to(f / total, (LANES, LANES)))
            spread = unstacked(weight)
            term = spread * part[:, p * LANES : (p + 1) * LANES].astype(full)
            value = term if value is None else value + term
        answer[:, p * LANES : (p + 1) * LANES] = value


def fill_bias(scalars, bias, rows):
    base, length, count = scalars[0], scalars[1], scalars[3]
    raw = rows + WIN
    pooled = rows // STRIDE + 2 * pool_half

    def block(first, size, valid):
        key = lax.broadcasted_iota(jnp.int32, (size, rows), 0)
        row = lax.broadcasted_iota(jnp.int32, (size, rows), 1)
        bias[pl.ds(first, size), :] = jnp.where(valid(key, row), 0.0, masked_score)

    def raw_valid(key, row):
        place = base - half + key
        near = (key >= row) & (key < row + WIN)
        return near & (place >= 0) & (place < length)

    def pool_valid(key, row):
        place = STRIDE * (key - pool_half)
        near = (place >= row - PWIN // 2) & (place < row + PWIN // 2)
        return near & (base + place >= 0) & (base + place < length)

    def quest_valid(key, row):
        return key < count

    block(0, raw, raw_valid)
    block(raw, pooled, pool_valid)
    block(raw + pooled, QMAX, quest_valid)


def collect(rows, width, qkv, pooled, everything, of):
    raw = rows + WIN
    count = rows // STRIDE + 2 * pool_half
    first = TAIL + rows - half
    quest = TAIL + 3 * rows
    everything[pl.ds(0, raw), :] = qkv[pl.ds(first, raw), of * width : (of + 1) * width]
    everything[pl.ds(raw, count), :] = pooled[:, (of - 1) * width : of * width]
    everything[pl.ds(raw + count, QMAX), :] = qkv[pl.ds(quest, QMAX), of * width : (of + 1) * width]


def lane_masks(rows):
    lane = lax.broadcasted_iota(jnp.int32, (rows, LANES), 1)
    return lane < DH


def only(block, first, keep):
    return jnp.where(first if keep == 0 else jnp.logical_not(first), block, jnp.zeros_like(block))


def stacked(block):
    first = lane_masks(block.shape[0])
    return jnp.concatenate([only(block, first, 0), only(block, first, 1)], axis=0)


def unstacked(block):
    lane = lax.broadcasted_iota(jnp.int32, (QMAX, LANES), 1)
    return jnp.where(lane < DH, block[:QMAX], block[QMAX:])


def attend_kernel(rows, width, devices, live, scalars, qkv, taps, local, pooled, stats, answer,
                  merged, wide, keys, values, bias, numerator, qstats, numerators, many, send_sem,
                  recv_sem):
    pairs = width // LANES
    own = TAIL + rows
    quest = TAIL + 3 * rows
    count = pooled.shape[0]
    begin = own - PWIN // 2 - taps.shape[0] // 2
    qstats[...] = jnp.zeros_like(qstats)

    def ask(p, carry):
        lanes = pl.ds(pl.multiple_of(p * LANES, LANES), LANES)
        question = stacked(qkv[pl.ds(quest, QMAX), lanes] * scale)
        own_key = qkv[pl.ds(own, rows), pl.ds(pl.multiple_of(width + p * LANES, LANES), LANES)]
        own_value = qkv[pl.ds(own, rows), pl.ds(pl.multiple_of(2 * width + p * LANES, LANES), LANES)]
        score = nt(own_key, question)
        top = jnp.max(score, axis=0, keepdims=True)
        weight = jnp.exp(score - top)
        qstats[pl.ds(2 * p, 1), :] = top
        qstats[pl.ds(2 * p + 1, 1), :] = jnp.sum(weight, axis=0, keepdims=True)
        numerator[:, lanes] = unstacked(jnp.transpose(tn(own_value, weight.astype(low)))).astype(low)
        return carry

    lax.fori_loop(0, pairs, ask, 0)
    pieces = ((numerator, numerators), (qstats, many))
    begin_all(devices, live, pieces, send_sem, recv_sem)

    def pool(p, carry):
        lanes = pl.ds(pl.multiple_of(p * LANES, LANES), LANES)
        wide[...] = qkv[pl.ds(0, quest), pl.ds(pl.multiple_of(width + p * LANES, LANES), LANES)].astype(full)
        total = None
        for tap in range(taps.shape[0]):
            term = taps[tap : tap + 1, lanes] * wide[pl.ds(begin + tap, count, stride=STRIDE), :]
            total = term if total is None else total + term
        pooled[:, lanes] = total.astype(low)
        return carry

    lax.fori_loop(0, 2 * pairs, pool, 0)
    collect(rows, width, qkv, pooled, keys, 1)
    collect(rows, width, qkv, pooled, values, 2)
    fill_bias(scalars, bias, rows)
    stats[...] = jnp.zeros_like(stats)
    first = lane_masks(rows)

    def pair(p, carry):
        lanes = pl.ds(pl.multiple_of(p * LANES, LANES), LANES)
        query = qkv[pl.ds(own, rows), lanes] * scale
        key = keys[:, lanes]
        value_t = jnp.transpose(values[:, lanes])
        parts = []
        for head in range(2):
            score = nt(key, only(query, first, head)) + bias[...]
            top = jnp.max(score, axis=0, keepdims=True)
            weight = jnp.exp(score - top)
            total = jnp.sum(weight, axis=0, keepdims=True)
            stats[pl.ds(2 * p + head, 1), :] = top + jnp.log(total)
            parts.append(mm(value_t[head * DH : (head + 1) * DH], weight.astype(low)) / total)
        local[:, lanes] = jnp.transpose(jnp.concatenate(parts, axis=0))
        return carry

    lax.fori_loop(0, pairs, pair, 0)
    finish_all(devices, live, pieces, send_sem, recv_sem)
    merge_questions(numerator, qstats, numerators, many, answer, merged)


def vmem_call(kernel, ident, copies, out_shapes, scratch, scalars, *inputs):
    vmem = pl.BlockSpec(memory_space=pltpu.VMEM)
    return pl.pallas_call(
        kernel,
        out_shape=[jax.ShapeDtypeStruct(s, t) for s, t in out_shapes],
        in_specs=[pl.BlockSpec(memory_space=pltpu.SMEM)] + [vmem] * len(inputs),
        out_specs=[vmem] * len(out_shapes),
        scratch_shapes=[pltpu.VMEM(s, t) for s, t in scratch]
        + [pltpu.SemaphoreType.DMA((copies,))] * 2,
        compiler_params=pltpu.CompilerParams(
            collective_id=ident, has_side_effects=True, vmem_limit_bytes=60 << 20
        ),
    )(scalars, *inputs)


def attend(ident, live, scalars, qkv, taps, rows):
    width = qkv.shape[1] // 3
    devices = lax.axis_size(SEQ)
    heads = width // DH
    pooled = rows // STRIDE + 2 * pool_half
    keys = rows + WIN + pooled + QMAX
    tall = -(-heads // 8) * 8
    return vmem_call(
        functools.partial(attend_kernel, rows, width, devices, live),
        ident,
        2 * (devices - 1),
        (
            ((rows, width), full),
            ((pooled, 2 * width), low),
            ((tall, rows), full),
            ((QMAX, width), full),
            ((tall, LANES), full),
        ),
        (
            ((TAIL + 3 * rows, LANES), full),
            ((keys, width), low),
            ((keys, width), low),
            ((keys, rows), full),
            ((QMAX, width), low),
            ((tall, LANES), full),
            ((devices - 1, QMAX, width), low),
            ((devices - 1, tall, LANES), full),
        ),
        scalars,
        qkv,
        taps,
    )


def attend_back_kernel(rows, width, devices, live, scalars, qkv, taps, pooled, stats, qstats, answer,
                       grad_mixed, grad_part, grads, grad_taps, wide, gwide, keys, values, gkeys,
                       gvalues, bias, grad_answer, grad_parts, send_sem, recv_sem):
    pieces = ((grad_part, grad_parts),)
    begin_all(devices, live, pieces, send_sem, recv_sem)
    pairs = width // LANES
    own = TAIL + rows
    quest = TAIL + 3 * rows
    raw = rows + WIN
    count = pooled.shape[0]
    begin = own - PWIN // 2 - taps.shape[0] // 2
    collect(rows, width, qkv, pooled, keys, 1)
    collect(rows, width, qkv, pooled, values, 2)
    fill_bias(scalars, bias, rows)
    first = lane_masks(rows)
    base, length, start, limit = scalars[0], scalars[1], scalars[2], scalars[3]
    place = base + lax.broadcasted_iota(jnp.int32, (rows, LANES), 0)
    plain = (place < start) | (place >= start + limit)
    grads[:, 0:width] = jnp.zeros((grads.shape[0], width), low)

    def pair(p, carry):
        lanes = pl.ds(pl.multiple_of(p * LANES, LANES), LANES)
        query = qkv[pl.ds(own, rows), lanes] * scale
        grad = jnp.where(plain, grad_mixed[:, lanes], jnp.zeros((rows, LANES), low))
        key = keys[:, lanes]
        value = values[:, lanes]
        key_t = jnp.transpose(key)
        parts = []
        gkey = None
        gvalue = None
        for head in range(2):
            one = only(query, first, head)
            out = only(grad, first, head)
            score = nt(key, one) + bias[...]
            soft = jnp.exp(score - stats[pl.ds(2 * p + head, 1), :])
            grad_soft = nt(value, out)
            delta = jnp.sum(soft * grad_soft, axis=0, keepdims=True)
            grad_score = (soft * (grad_soft - delta)).astype(low)
            more_v = mm(soft.astype(low), out)
            more_k = mm(grad_score, one)
            gvalue = more_v if gvalue is None else gvalue + more_v
            gkey = more_k if gkey is None else gkey + more_k
            parts.append(mm(key_t[head * DH : (head + 1) * DH], grad_score))
        grads[pl.ds(own, rows), lanes] = (
            jnp.transpose(jnp.concatenate(parts, axis=0)) * scale
        ).astype(low)
        gkeys[:, lanes] = gkey
        gvalues[:, lanes] = gvalue
        return carry

    lax.fori_loop(0, pairs, pair, 0)
    finish_all(devices, live, pieces, send_sem, recv_sem)
    grad_answer[...] = slot_sum(grad_part[...], grad_parts).astype(low)

    def ask(p, carry):
        lanes = pl.ds(pl.multiple_of(p * LANES, LANES), LANES)
        question = stacked(qkv[pl.ds(quest, QMAX), lanes] * scale)
        grad_q = grad_answer[:, lanes]
        out = stacked(grad_q)
        own_key = keys[pl.ds(half, rows), lanes]
        own_value = values[pl.ds(half, rows), lanes]
        score = nt(own_key, question)
        soft = jnp.exp(score - qstats[pl.ds(2 * p, 1), :])
        grad_soft = nt(own_value, out)
        product = stacked(grad_q.astype(full) * answer[:, lanes])
        delta = jnp.sum(jnp.transpose(product), axis=0, keepdims=True)
        grad_score = (soft * (grad_soft - delta)).astype(low)
        grads[pl.ds(quest, QMAX), lanes] = (
            unstacked(jnp.transpose(tn(own_key, grad_score))) * scale
        ).astype(low)
        gkeys[pl.ds(half, rows), lanes] += mm(grad_score, question)
        gvalues[pl.ds(half, rows), lanes] += mm(soft.astype(low), out)
        return carry

    lax.fori_loop(0, pairs, ask, 0)
    spot = base - own + lax.broadcasted_iota(jnp.int32, (quest, LANES), 0)
    inside = (spot >= 0) & (spot < length)
    tail = quest - (own - half) - raw

    def unpool(part, at, p):
        lanes = pl.ds(pl.multiple_of(p * LANES, LANES), LANES)
        tapped = pl.ds(pl.multiple_of(at - width + p * LANES, LANES), LANES)
        target = pl.ds(pl.multiple_of(at + p * LANES, LANES), LANES)
        wide[...] = qkv[pl.ds(0, quest), target].astype(full)
        gwide[pl.ds(0, own - half), :] = jnp.zeros((own - half, LANES), full)
        gwide[pl.ds(own - half, raw), :] = part[pl.ds(0, raw), lanes]
        gwide[pl.ds(quest - tail, tail), :] = jnp.zeros((tail, LANES), full)
        gpool = part[pl.ds(raw, count), lanes]
        for tap in range(taps.shape[0]):
            near = pl.ds(begin + tap, count, stride=STRIDE)
            gwide[near, :] += taps[tap : tap + 1, tapped] * gpool
            grad_taps[tap : tap + 1, tapped] = jnp.sum(gpool * wide[near, :], axis=0, keepdims=True)
        grads[pl.ds(0, quest), target] = jnp.where(inside, gwide[...], 0.0).astype(low)
        grads[pl.ds(quest, QMAX), target] = part[pl.ds(raw + count, QMAX), lanes].astype(low)

    def both(p, carry):
        unpool(gkeys, width, p)
        unpool(gvalues, 2 * width, p)
        return carry

    lax.fori_loop(0, pairs, both, 0)


def attend_back(ident, live, scalars, qkv, taps, pooled, stats, qstats, answer, grad_mixed,
                grad_part, rows):
    width = qkv.shape[1] // 3
    devices = lax.axis_size(SEQ)
    count = rows // STRIDE + 2 * pool_half
    keys = rows + WIN + count + QMAX
    span = TAIL + 3 * rows
    return vmem_call(
        functools.partial(attend_back_kernel, rows, width, devices, live),
        ident,
        devices - 1,
        ((qkv.shape, low), (taps.shape, full)),
        (
            ((span, LANES), full),
            ((span, LANES), full),
            ((keys, width), low),
            ((keys, width), low),
            ((keys, width), full),
            ((keys, width), full),
            ((keys, rows), full),
            ((QMAX, width), low),
            ((devices - 1, QMAX, width), low),
        ),
        scalars,
        qkv,
        taps,
        pooled,
        stats,
        qstats,
        answer,
        grad_mixed,
        grad_part,
    )


def reduce_kernel(count, blocks, side, across, n_in, live, *refs):
    ins, refs = refs[:n_in], refs[n_in:]
    tap_grads, vectors, refs = refs[0], refs[1:5], refs[5:]
    outs, little_out, refs = refs[:n_in], refs[n_in], refs[n_in + 1 :]
    first_in, second_in, across_in, little_in, little_slots, little_x, little_y = refs[:7]
    held, made = refs[7:9]
    one, two, over, back, back_two, back_one, tiny, load, store_sem = refs[9:]
    total = len(blocks)
    big, small = side // 2, side // 4
    piece = max(TAIL, small // count)
    owners = small // piece
    me = lax.axis_index(SEQ)
    place = lax.axis_index(DP)
    bit_x, bit_y = lax.rem(place, 2), place // 2
    to_x, to_y = place + 1 - 2 * bit_x, place + 2 - 4 * bit_y

    def ways(b):
        if b % 2 == 0:
            return bit_x, bit_y, to_x, to_y
        return bit_y, bit_x, to_y, to_x

    def view(group, b, row, rows):
        ref, top, left = blocks[b]
        row = pl.multiple_of(top + row, TAIL)
        return group[ref].at[pl.ds(row, rows), left : left + across]

    def final(b, row, rows):
        return made.at[b, pl.ds(pl.multiple_of(row, TAIL), rows)]

    def fetch(b):
        f, s, near, far = ways(b)
        return pltpu.make_async_copy(view(ins, b, f * big, big), held.at[b], load.at[b])

    def keep(b):
        return pltpu.make_async_copy(made.at[b], view(outs, b, 0, side), store_sem.at[b])

    def remote(src, dst, sems, index, axis, peer):
        return pltpu.make_async_remote_copy(
            src_ref=src,
            dst_ref=dst,
            send_sem=sems.at[(0,) + index],
            recv_sem=sems.at[(1,) + index],
            device_id={axis: peer},
            device_id_type=MESH,
        )

    def stage_one(b):
        f, s, near, far = ways(b)
        return remote(view(ins, b, (1 - f) * big, big), first_in.at[b], one, (b,), DP, near)

    def stage_two(b):
        f, s, near, far = ways(b)
        row = pl.multiple_of((1 - s) * small, TAIL)
        return remote(first_in.at[b, pl.ds(row, small)], second_in.at[b], two, (b,), DP, far)

    def spread(b, step):
        peer = lax.rem(me + step, count)
        row = pl.multiple_of(jnp.minimum(peer, owners - 1) * piece, TAIL)
        copy = remote(
            second_in.at[b, pl.ds(row, piece)], across_in.at[b, step - 1], over, (b, step - 1), SEQ, peer
        )
        return copy, peer < owners, me < owners

    def mine(b):
        f, s, near, far = ways(b)
        return f * big + s * small

    def gather(b, step):
        peer = lax.rem(me + step, count)
        row = mine(b) + jnp.minimum(me, owners - 1) * piece
        here = final(b, row, piece)
        copy = remote(here, here, back, (b, step - 1), SEQ, peer)
        return copy, me < owners, lax.rem(me + count - step, count) < owners

    def gather_two(b):
        f, s, near, far = ways(b)
        here = final(b, mine(b), small)
        return remote(here, here, back_two, (b,), DP, far)

    def gather_one(b):
        f, s, near, far = ways(b)
        here = final(b, f * big, big)
        return remote(here, here, back_one, (b,), DP, near)

    def guarded(condition, action):
        if owners == count:
            action()
        else:
            pl.when(condition)(action)

    def begin_one(b):
        stage_one(b).start()
        fetch(b).start()

    def finish_one(b):
        f, s, near, far = ways(b)
        fetch(b).wait()
        stage_one(b).wait_recv()
        own = held[b].astype(full)
        first_in[b] = (first_in[b].astype(full) + own).astype(low)
        stage_two(b).start()

    def finish_two(b):
        f, s, near, far = ways(b)
        stage_two(b).wait_recv()
        own = first_in[b, pl.ds(pl.multiple_of(s * small, TAIL), small)].astype(full)
        second_in[b] = (second_in[b].astype(full) + own).astype(low)
        for step in range(1, count):
            copy, send, take = spread(b, step)
            guarded(send, copy.start)

    def finish_over(b):
        for step in range(1, count):
            copy, send, take = spread(b, step)
            guarded(take, copy.wait_recv)

        def store():
            row = pl.multiple_of(jnp.minimum(me, owners - 1) * piece, TAIL)
            answer = second_in[b, pl.ds(row, piece)].astype(full)
            for step in range(1, count):
                answer = answer + across_in[b, step - 1].astype(full)
            final(b, mine(b) + row, piece)[...] = answer.astype(low)

        guarded(me < owners, store)
        for step in range(1, count):
            copy, send, take = gather(b, step)
            guarded(send, copy.start)

    def finish_back(b):
        for step in range(1, count):
            copy, send, take = gather(b, step)
            guarded(take, copy.wait_recv)
        gather_two(b).start()

    def finish_back_two(b):
        gather_two(b).wait_recv()
        gather_one(b).start()

    def finish_back_one(b):
        gather_one(b).wait_recv()
        keep(b).start()

    def little_copy(step):
        peer = lax.rem(me + step, count)
        return remote(little_in, little_slots.at[step - 1], tiny, (step - 1,), SEQ, peer)

    def little_pair(slot, src, dst, peer):
        return remote(src, dst, tiny, (count - 1 + slot,), DP, peer)

    @pl.when(lax.axis_index(SECTION) == live)
    def _():
        barrier = pltpu.get_barrier_semaphore()
        for step in range(1, count):
            peer = lax.rem(me + step, count)
            pl.semaphore_signal(barrier, inc=1, device_id={SEQ: peer}, device_id_type=MESH)
        for peer in (to_x, to_y):
            pl.semaphore_signal(barrier, inc=1, device_id={DP: peer}, device_id_type=MESH)
        pl.semaphore_wait(barrier, count + 1)

        taps = tap_grads.shape[0]
        little_in[...] = jnp.zeros_like(little_in)
        little_in[0:taps, :] = tap_grads[:, :side]
        little_in[taps : 2 * taps, :] = tap_grads[:, side:]
        for k, vector in enumerate(vectors):
            little_in[2 * taps + k : 2 * taps + k + 1, :] = vector[...]
        for step in range(1, count):
            little_copy(step).start()
        pairs = total // 2
        ahead = 3
        stages = (finish_one, finish_two, finish_over, finish_back, finish_back_two, finish_back_one)
        for k in range(min(ahead, pairs)):
            begin_one(2 * k)
            begin_one(2 * k + 1)
        for turn in range(pairs + len(stages) - 1):
            for depth, stage in enumerate(stages):
                k = turn - depth
                if 0 <= k < pairs:
                    stage(2 * k)
                    stage(2 * k + 1)
                if depth == 0 and turn + ahead < pairs:
                    begin_one(2 * (turn + ahead))
                    begin_one(2 * (turn + ahead) + 1)
            if turn == 0:
                for step in range(1, count):
                    little_copy(step).wait()
                value = little_in[...]
                for step in range(1, count):
                    value = value + little_slots[step - 1]
                little_x[0] = value
                little_pair(0, little_x.at[0], little_x.at[1], to_x).start()
            if turn == 1:
                little_pair(0, little_x.at[0], little_x.at[1], to_x).wait()
                little_y[0] = little_x[0] + little_x[1]
                little_pair(1, little_y.at[0], little_y.at[1], to_y).start()
            if turn == 2:
                little_pair(1, little_y.at[0], little_y.at[1], to_y).wait()
                little_out[...] = little_y[0] + little_y[1]
        for b in range(total):
            stage_one(b).wait_send()
            stage_two(b).wait_send()
            for step in range(1, count):
                copy, send, take = spread(b, step)
                guarded(send, copy.wait_send)
                copy, send, take = gather(b, step)
                guarded(send, copy.wait_send)
            gather_two(b).wait_send()
            gather_one(b).wait_send()
            keep(b).wait()


def unwritten(shapes):
    return pl.pallas_call(
        lambda *refs: None,
        out_shape=[jax.ShapeDtypeStruct(shape, low) for shape in shapes],
        out_specs=[pl.BlockSpec(memory_space=pl.ANY)] * len(shapes),
    )()


def reduce_all(parts, little, ident, live):
    count = lax.axis_size(SEQ)
    tall = -(-(2 * little[0].shape[0] + len(little) - 1) // 8) * 8
    side = min(min(part.shape) for part in parts)
    across = side // 2
    blocks = []
    for k, part in enumerate(parts):
        for top in range(0, part.shape[0], side):
            for left in range(0, part.shape[1], across):
                blocks.append((k, top, left))
    total = len(blocks)
    small = side // 4
    piece = max(TAIL, small // count)
    vmem = pl.BlockSpec(memory_space=pltpu.VMEM)
    sems = pltpu.SemaphoreType.DMA
    return pl.pallas_call(
        functools.partial(reduce_kernel, count, blocks, side, across, len(parts), live),
        out_shape=[jax.ShapeDtypeStruct(part.shape, low) for part in parts]
        + [jax.ShapeDtypeStruct((tall, side), full)],
        in_specs=[pl.BlockSpec(memory_space=pl.ANY)] * len(parts) + [vmem] * len(little),
        out_specs=[pl.BlockSpec(memory_space=pl.ANY)] * len(parts) + [vmem],
        scratch_shapes=[
            pltpu.VMEM((total, side // 2, across), low),
            pltpu.VMEM((total, small, across), low),
            pltpu.VMEM((total, count - 1, piece, across), low),
            pltpu.VMEM((tall, side), full),
            pltpu.VMEM((count - 1, tall, side), full),
            pltpu.VMEM((2, tall, side), full),
            pltpu.VMEM((2, tall, side), full),
            pltpu.VMEM((total, side // 2, across), low),
            pltpu.VMEM((total, side, across), low),
            sems((2, total)),
            sems((2, total)),
            sems((2, total, count - 1)),
            sems((2, total, count - 1)),
            sems((2, total)),
            sems((2, total)),
            sems((2, count + 1)),
            sems((total,)),
            sems((total,)),
        ],
        compiler_params=pltpu.CompilerParams(
            collective_id=ident, has_side_effects=True, vmem_limit_bytes=62 << 20
        ),
    )(*parts, *little)


def layer_forward(tick, live, state_low, params, positions, count):
    qkv_w, output_w, up_w, down_w, taps, gain_one, bias_one, gain_two, bias_two = params
    rows, width = state_low.shape
    base = lax.axis_index(SEQ) * rows
    length = lax.axis_size(SEQ) * rows
    valid = jnp.arange(QMAX, dtype=jnp.int32) < count
    row_pos = base + jnp.arange(rows, dtype=jnp.int32)
    select = (positions[:, None] == row_pos[None, :]) & valid[:, None]
    select_low = select.astype(low)
    scalars = jnp.stack([base, jnp.int32(length), positions[0], count])
    pick = mm(select_low, state_low).astype(low)
    extended = gather_rows(4 * tick, live, state_low, pick)
    normed = norm_rows(extended.astype(full), gain_one, bias_one).astype(low)
    spot = base - TAIL - rows + jnp.arange(extended.shape[0], dtype=jnp.int32)
    inside = ((spot >= 0) & (spot < length)) | (jnp.arange(extended.shape[0]) >= TAIL + 3 * rows)
    qkv = jnp.where(inside[:, None], mm(normed, qkv_w), 0.0).astype(low)
    local, pooled, stats, answer, qstats = attend(4 * tick + 1, live, scalars, qkv, taps, rows)
    is_question = jnp.any(select, axis=0)
    replaced = tn(select_low, answer.astype(low))
    mixed = jnp.where(is_question[:, None], replaced, local).astype(low)
    state = state_low.astype(full)
    middle = state + mm(mixed, output_w)
    normed_two = norm_rows(middle, gain_two, bias_two).astype(low)
    hidden = mm(normed_two, up_w)
    active, slope = gelu_parts(hidden)
    result = middle + mm(active, down_w)
    tape = (state_low, select_low, scalars, normed, qkv, pooled, stats, qstats, answer, mixed,
            middle, normed_two, slope, active)
    return result.astype(low), tape


def layer_backward(tick, live, grad_low, params, tape):
    qkv_w, output_w, up_w, down_w, taps, gain_one, bias_one, gain_two, bias_two = params
    (state_low, select_low, scalars, normed, qkv, pooled, stats, qstats, answer, mixed,
     middle, normed_two, slope, active) = tape
    rows, width = state_low.shape
    grad_out = grad_low.astype(full)
    grad_active = nt(grad_low, down_w)
    grad_hidden = (grad_active * slope.astype(full)).astype(low)
    grad_normed_two = nt(grad_hidden, up_w)
    _, norm_back_two = jax.vjp(norm_rows, middle, gain_two, bias_two)
    grad_middle, g_gain_two, g_bias_two = norm_back_two(grad_normed_two)
    grad_middle = grad_middle + grad_out
    branch = grad_middle.astype(low)
    grad_mixed = nt(branch, output_w).astype(low)
    grad_part = mm(select_low, grad_mixed).astype(low)
    grads, grad_taps = attend_back(
        4 * tick + 2, live, scalars, qkv, taps, pooled, stats, qstats, answer, grad_mixed,
        grad_part, rows
    )
    grad_extended = nt(grads, qkv_w).astype(low)
    grad_normed, grad_picked = return_rows(4 * tick + 3, live, grad_extended, rows)
    grad_normed = grad_normed + tn(select_low, grad_picked.astype(low))
    _, norm_back_one = jax.vjp(norm_rows, state_low.astype(full), gain_one, bias_one)
    grad_state, g_gain_one, g_bias_one = norm_back_one(grad_normed)
    small = (grad_taps, g_gain_one, g_bias_one, g_gain_two, g_bias_two)
    big = ((normed, grads), (mixed, branch), (normed_two, grad_hidden), (active, grad_low))
    return (grad_state + grad_middle).astype(low), big, small


def to_partner(block):
    return lax.ppermute(block, SECTION, [(0, 1), (1, 0)])


def per_device(
    inputs,
    cotangent,
    question_positions,
    question_counts,
    query_weight,
    key_weight,
    value_weight,
    output_weight,
    up_weight,
    down_weight,
    key_pool,
    value_pool,
    attn_norm_gain,
    attn_norm_bias,
    ffn_norm_gain,
    ffn_norm_bias,
):
    params = (
        jnp.concatenate([query_weight[0], key_weight[0], value_weight[0]], axis=1),
        output_weight[0],
        up_weight[0],
        down_weight[0],
        jnp.concatenate([key_pool[0], value_pool[0]], axis=1),
        attn_norm_gain[0],
        attn_norm_bias[0],
        ffn_norm_gain[0],
        ffn_norm_bias[0],
    )
    section = lax.axis_index(SECTION)
    micro, rows, width = inputs.shape

    def alive(tick):
        if tick == 0:
            return 0
        return 1 if tick == micro else None

    received = jnp.zeros((rows, width), low)
    tapes = []
    made = []
    for tick in range(micro + 1):
        slot = jnp.clip(tick - section, 0, micro - 1)
        layer_in = jnp.where(section == 0, inputs[min(tick, micro - 1)], received)
        result, tape = layer_forward(
            tick, alive(tick), layer_in, params, question_positions[slot], question_counts[slot]
        )
        tapes.append(tape)
        made.append(result)
        if tick < micro:
            received = to_partner(result)
    produced = jnp.where(section == 0, jnp.stack(made[:micro]), jnp.stack(made[1:]))
    grad_in = jnp.zeros((rows, width), low)
    back = []
    bigs = []
    smalls = []
    reduced = []

    def reduce_section(which):
        ticks = range(1 - which, micro + 1 - which)

        def sums():
            parts = []
            for k in range(len(bigs[0])):
                left = jnp.concatenate([bigs[t][k][0] for t in ticks], axis=0)
                right = jnp.concatenate([bigs[t][k][1] for t in ticks], axis=0)
                parts.append(tn(left, right).astype(low))
            return parts

        def nothing():
            return list(unwritten([(a.shape[1], b.shape[1]) for a, b in bigs[micro - 1]]))

        parts = lax.cond(section == which, sums, nothing)
        little = []
        for k in range(len(smalls[0])):
            total = smalls[ticks[0]][k]
            for t in ticks[1:]:
                total = total + smalls[t][k]
            little.append(total.reshape(-1, total.shape[-1]))
        reduced.append(reduce_all(parts, little, 4 * micro + 4 + which, which))

    for tick in range(micro + 1):
        mirror = micro - tick
        grad_out = jnp.where(section == 1, cotangent[max(mirror - 1, 0)], grad_in)
        grad_state, big, small = layer_backward(
            mirror, alive(mirror), grad_out, params, tapes[mirror]
        )
        back.append(grad_state)
        bigs.append(big)
        smalls.append(small)
        if tick < micro:
            grad_in = to_partner(grad_state)
        if tick == micro - 1:
            grad_in, bigs, smalls = lax.optimization_barrier((grad_in, bigs, smalls))
            reduce_section(1)
            grad_in, reduced[0] = lax.optimization_barrier((grad_in, reduced[0]))
    back_grads = jnp.where(
        section == 0, jnp.stack(back[1:][::-1]), jnp.stack(back[:micro][::-1])
    )
    reduce_section(0)
    *sums, little = [
        jnp.where(section == 0, mine, other).astype(full) for other, mine in zip(*reduced)
    ]
    taps = key_pool.shape[1]
    return (
        produced[None],
        back_grads[None],
        sums[0][None, :, :width],
        sums[0][None, :, width : 2 * width],
        sums[0][None, :, 2 * width :],
        sums[1][None],
        sums[2][None],
        sums[3][None],
        little[None, :taps],
        little[None, taps : 2 * taps],
        little[2 * taps : 2 * taps + 1],
        little[2 * taps + 1 : 2 * taps + 2],
        little[2 * taps + 2 : 2 * taps + 3],
        little[2 * taps + 3 : 2 * taps + 4],
    )


def solution(mesh):
    rows = P(DP, SEQ, None)
    matrix = P(SECTION, None, None)
    vector = P(SECTION, None)
    result = P(SECTION, DP, SEQ, None)
    return jax.shard_map(
        per_device,
        mesh=mesh,
        in_specs=(rows, rows, P(DP, None), P(DP)) + (matrix,) * 8 + (vector,) * 4,
        out_specs=(result, result) + (matrix,) * 8 + (vector,) * 4,
        check_vma=False,
    )
```

time: 1480 us -> 626 us (0.42)
  waiting for transfers between devices: 500 us -> 2.51 us
  Pallas kernels: 0 us -> 377 us
  local copies, waits for them, and re-layouts: 278 us -> 20.9 us
  blocking collectives: 162 us -> 0 us
  matrix products: 278 us -> 129 us
  other arithmetic: 143 us -> 57.4 us
  starting transfers between devices: 82.2 us -> 27.3 us
  between operations: 18.7 us -> 3.18 us
    psum x13 -> x0, waiting for transfers between devices: 498 us -> none  [the longest x1 287 us: per_device(): lax.psum(tuple((part.astype(jnp.bfloat16) for part in flat)), ('dp', 'seq'))]
    pallas_call x0 -> x15, Pallas kernels: none -> 377 us  [the longest x2 177 us: reduce_all(): pl.pallas_call(functools.partial(reduce_kernel, count, blocks, side, acro...]
    dot_general x105 -> x40, matrix products: 255 us -> 129 us  [the longest x18 50.7 us: mm(): return jnp.dot(left, right, preferred_element_type=full)]
    slice x77 -> x1, local copies, waits for them, and re-layouts: 92.7 us -> 0.6 us  [per_device(): little[2 * taps + 3:2 * taps + 4]]
    reshape x61 -> x8, local copies, waits for them, and re-layouts: 88.5 us -> 4.66 us  [reduce_section(): little.append(total.reshape(-1, total.shape[-1]))]
    psum x1 -> x0, blocking collectives: 82.2 us -> none  [per_device(): lax.psum(tuple((part.astype(jnp.bfloat16) for part in flat)), ('dp', 'seq'))]
    all_gather x6 -> x0, blocking collectives: 79.9 us -> none  [merged(): everything = jax.tree.map(lambda part: lax.all_gather(part, axis), shard)]
    ppermute x28 -> x4, starting transfers between devices: 80.7 us -> 27.3 us  [to_partner(): return lax.ppermute(block, SECTION, [(0, 1), (1, 0)])]
  transfers between devices with their start and end apart: 41 -> 4, of which waited for: 13 -> 2; matrix products, arithmetic and copies ran while one was open for 23% -> 2% of each run, Pallas kernels for 0% -> 0%
where the time goes in v1:
time: 626 us; the launch traced here: 617 us
  Pallas kernels  377 us (60%)
  matrix products  129 us (21%)
  other arithmetic  57.4 us (9%)
  starting transfers between devices  27.3 us (4%)
  local copies, waits for them, and re-layouts  20.9 us (3%)
    pallas_call x2, Pallas kernels, reduce_all(): pl.pallas_call(functools.partial(reduce_kernel, count, blocks, side, acro...  177 us
    pallas_call x6, Pallas kernels, vmem_call(): pl.pallas_call(kernel, out_shape=[jax.ShapeDtypeStruct(s, t) for s, t in...  116 us
    pallas_call x6, Pallas kernels, exchange(): pl.pallas_call(kernel, out_shape=[jax.ShapeDtypeStruct(s, t) for s, t in...  84.4 us
    dot_general x18, matrix products, mm(): return jnp.dot(left, right, preferred_element_type=full)  50.7 us
    dot_general x12, matrix products, nt(): lax.dot_general(left, right, (((1,), (1,)), ((), ())), preferred_element_...  44.8 us
    dot_general x10, matrix products, tn(): lax.dot_general(left, right, (((0,), (0,)), ((), ())), preferred_element_...  33.5 us
    ppermute x4, starting transfers between devices, to_partner(): return lax.ppermute(block, SECTION, [(0, 1), (1, 0)])  27.3 us
  transfers between devices with their start and end apart: 4, of which 2 were waited for; matrix products, arithmetic and copies ran while one was open for 2% of the time, Pallas kernels for 0%

profile of v1, /device:TPU:0, one launch (start us, length us, event | category | flops | bytes accessed | tf_op | source)
XLA Modules:
  0.0 617.3 jit_solution(9758244060181324976)
XLA Ops:
  0.7 1.4 fusion.262
  3.6 1.7 convert_reduce_fusion.5
  6.2 16.7 %shard_map.263 = bf16[848,768]{1,0:T(8,128)(2,1)} custom-call(bf16[256,768]{1,0:T(8,128)(2,1)} %copy-done.4, bf16[64,768]{1,0:T(8,128)(2,1)} %convolution_convert_fusion.17.refs_1_), custom_call_target="tpu_custom_call" | custom-call | tf_op jit(solution)/shard_map/pallas_call | solution.py:139
  24.4 1.6 convert_reduce_fusion.2
  26.0 1.8 fusion.135
  28.6 1.3 iota_compare_fusion.1
  30.5 2.0 pad_add_fusion
  32.5 7.2 %select_convert_fusion.2.qkv = bf16[848,2304]{1,0:T(8,128)(2,1)} fusion(bf16[848,768]{1,0:T(8,128)(2,1)S(1)} %fusion.138, pred[848]{0:T(1024)(128)(4,1)S(1)} %fusion.245, bf16[768,768]{1,0:T(8,128)(2,1)} %bitcast.214, bf16[768,768]{1,0:T(8,128)(2,1)} %bitcast.220, bf16[768,768]{1,0:T(8,128)(2,1)} %bitcast.226), kind=kOutput, calls=%fused_computation.68 | convolution fusion | flops 3015548928 | bytes 8749904 | tf_op jit(solution)/shard_map/dot_general | solution.py:44
  39.6 17.3 %shard_map.264 = (f32[256,768]{1,0:T(8,128)}, bf16[192,1536]{1,0:T(8,128)(2,1)}, f32[16,256]{1,0:T(8,128)}, f32[64,768]{1,0:T(8,128)}, f32[16,128]{1,0:T(8,128)}) custom-call(s32[4]{0:T(128)} %get-tuple-element.372.scalars, bf16[848,2304]{1,0:T(8,128)(2,1)} %select_convert_fusion.2.qkv, f32[5,1536]{1,0:T(8,128)} %pad_maximum_fusion.1.taps), custom_call_target="tpu_custom_call" | custom-call | tf_op jit(solution)/shard_map/pallas_call | solution.py:428
  57.7 1.6 fusion.157
  61.1 5.9 multiply_convert_fusion.2
  67.2 1.4 fusion.154
  68.7 1.7 collective-permute-done
  72.0 19.8 %shard_map.265 = bf16[848,768]{1,0:T(8,128)(2,1)} custom-call(bf16[256,768]{1,0:T(8,128)(2,1)} %copy-done.6, bf16[64,768]{1,0:T(8,128)(2,1)} %convolution_convert_fusion.16.refs_1_), custom_call_target="tpu_custom_call" | custom-call | tf_op jit(solution)/shard_map/pallas_call | solution.py:139
  91.9 1.7 convert_reduce_fusion.1
  93.6 1.9 fusion.131
  96.8 5.4 select_convert_fusion.1.qkv
  102.2 20.2 %shard_map.266 = (f32[256,768]{1,0:T(8,128)}, bf16[192,1536]{1,0:T(8,128)(2,1)}, f32[16,256]{1,0:T(8,128)}, f32[64,768]{1,0:T(8,128)}, f32[16,128]{1,0:T(8,128)}) custom-call(s32[4]{0:T(128)} %get-tuple-element.373.scalars, bf16[848,2304]{1,0:T(8,128)(2,1)} %select_convert_fusion.1.qkv, f32[5,1536]{1,0:T(8,128)} %pad_maximum_fusion.1.taps), custom_call_target="tpu_custom_call" | custom-call | tf_op jit(solution)/shard_map/pallas_call | solution.py:428
  122.4 1.6 fusion.158
  126.3 5.7 multiply_convert_fusion.1
  132.1 2.2 fusion.151
  134.2 1.9 pad_add_fusion.3.scalars
  137.7 1.6 convolution_convert_fusion.15.refs_1_
  139.3 2.8 shard_map.267
  142.2 1.7 convert_reduce_fusion
  143.9 1.9 fusion.127
  147.5 5.4 select_convert_fusion.qkv
  152.9 14.1 %shard_map.268 = (f32[256,768]{1,0:T(8,128)}, bf16[192,1536]{1,0:T(8,128)(2,1)}, f32[16,256]{1,0:T(8,128)}, f32[64,768]{1,0:T(8,128)}, f32[16,128]{1,0:T(8,128)}) custom-call(s32[4]{0:T(128)} %pad_add_fusion.3.scalars, bf16[848,2304]{1,0:T(8,128)(2,1)} %select_convert_fusion.qkv, f32[5,1536]{1,0:T(8,128)} %pad_maximum_fusion.1.taps), custom_call_target="tpu_custom_call" | custom-call | tf_op jit(solution)/shard_map/pallas_call | solution.py:428
  167.0 1.6 fusion.159
  170.5 6.0 multiply_convert_fusion
  176.6 2.0 fusion.103
  178.6 2.2 multiply_reduce_fusion.3
  183.5 19.3 %shard_map.269 = (bf16[848,2304]{1,0:T(8,128)(2,1)}, f32[5,1536]{1,0:T(8,128)}) custom-call(s32[4]{0:T(128)} %pad_add_fusion.3.scalars, bf16[848,2304]{1,0:T(8,128)(2,1)} %select_convert_fusion.qkv, f32[5,1536]{1,0:T(8,128)} %pad_maximum_fusion.1.taps, bf16[192,1536]{1,0:T(8,128)(2,1)} %get-tuple-element.200.pooled, f32[16,256]{1,0:T(8,128)} %get-tuple-element.201.stats, ...), custom_call_target="tpu_custom_call" | custom-call | tf_op jit(solution)/shard_map/pallas_call | solution.py:428
  202.9 7.4 %convolution_convert_fusion.8.refs_0_ = bf16[848,768]{1,0:T(8,128)(2,1)} fusion(bf16[848,2304]{1,0:T(8,128)(2,1)} %get-tuple-element.214, bf16[768,768]{1,0:T(8,128)(2,1)} %bitcast.215, bf16[768,768]{1,0:T(8,128)(2,1)} %bitcast.221, bf16[768,768]{1,0:T(8,128)(2,1)} %bitcast.227), kind=kOutput, calls=%fused_computation.156 | convolution fusion | flops 3012292608 | bytes 8749056 | tf_op jit(solution)/shard_map/dot_general | solution.py:52
  210.3 2.8 shard_map.270
  213.1 2.6 fusion.257
  217.1 27.1 %collective-permute-start.2 = (bf16[256,768]{1,0:T(8,128)(2,1)S(1)}, bf16[256,768]{1,0:T(8,128)(2,1)S(1)}, u32[]{:S(2)}, u32[]{:S(2)}) collective-permute-start(bf16[256,768]{1,0:T(8,128)(2,1)S(1)} %add_convert_fusion.2), channel_id=1, source_target_pairs={{0,16},{16,0},{1,17},{17,1},{2,18},{18,2},{3,19},{19,3},{4,20},{20... | collective-permute-start | bytes 1179656 | tf_op jit(solution)/shard_map/ppermute | solution.py:939
  245.7 4.3 fusion.100
  250.1 1.7 multiply_reduce_fusion.2
  254.6 22.0 %shard_map.271 = (bf16[848,2304]{1,0:T(8,128)(2,1)}, f32[5,1536]{1,0:T(8,128)}) custom-call(s32[4]{0:T(128)} %get-tuple-element.373.scalars, bf16[848,2304]{1,0:T(8,128)(2,1)} %select_convert_fusion.1.qkv, f32[5,1536]{1,0:T(8,128)} %pad_maximum_fusion.1.taps, bf16[192,1536]{1,0:T(8,128)(2,1)} %get-tuple-element.197.pooled, ...), custom_call_target="tpu_custom_call" | custom-call | tf_op jit(solution)/shard_map/pallas_call | solution.py:428
  276.6 7.4 %convolution_convert_fusion.7.refs_0_ = bf16[848,768]{1,0:T(8,128)(2,1)} fusion(bf16[848,2304]{1,0:T(8,128)(2,1)} %get-tuple-element.215, bf16[768,768]{1,0:T(8,128)(2,1)} %bitcast.216, bf16[768,768]{1,0:T(8,128)(2,1)} %bitcast.222, bf16[768,768]{1,0:T(8,128)(2,1)} %bitcast.228), kind=kOutput, calls=%fused_computation.155 | convolution fusion | flops 3012292608 | bytes 8749056 | tf_op jit(solution)/shard_map/dot_general | solution.py:52
  284.0 21.9 %shard_map.272 = (f32[256,768]{1,0:T(8,128)}, f32[64,768]{1,0:T(8,128)}, bf16[256,768]{1,0:T(8,128)(2,1)}, bf16[256,768]{1,0:T(8,128)(2,1)}, bf16[16,768]{1,0:T(8,128)(2,1)}) custom-call(bf16[848,768]{1,0:T(8,128)(2,1)} %convolution_convert_fusion.7.refs_0_), custom_call_target="tpu_custom_call" | custom-call | tf_op jit(solution)/shard_map/pallas_call | solution.py:139
  305.9 2.0 fusion.256
  309.0 3.9 fusion.160
  313.0 2.2 maximum_select_fusion
  318.9 6.5 %shard_map.273 = (bf16[768,2304]{1,0:T(8,128)(2,1)}, bf16[768,768]{1,0:T(8,128)(2,1)}, bf16[768,3072]{1,0:T(8,128)(2,1)}, bf16[3072,768]{1,0:T(8,128)(2,1)}, f32[16,768]{1,0:T(8,128)}) custom-call(bf16[768,2304]{1,0:T(8,128)(2,1)} %get-tuple-element.228.refs_0_, bf16[768,768]{1,0:T(8,128)(2,1)} %get-tuple-element.229.refs_1_, ...), custom_call_target="tpu_custom_call" | custom-call | tf_op jit(solution)/shard_map/pallas_call | solution.py:846
  326.6 6.4 %fusion.97 = bf16[256,3072]{1,0:T(8,128)(2,1)S(1)} fusion(bf16[256,768]{1,0:T(8,128)(2,1)S(1)} %bitcast_select_fusion, bf16[1,3072,768]{2,1,0:T(8,128)(2,1)} %param.29, f32[256,3072]{1,0:T(8,128)} %get-tuple-element.357), kind=kOutput, calls=%fused_computation.101 | convolution fusion | flops 1217396736 | bytes 9830400 | tf_op jit(solution)/shard_map/dot_general | solution.py:52
  333.0 4.6 multiply_reduce_fusion
  340.5 22.7 %shard_map.274 = (bf16[848,2304]{1,0:T(8,128)(2,1)}, f32[5,1536]{1,0:T(8,128)}) custom-call(s32[4]{0:T(128)} %get-tuple-element.372.scalars, bf16[848,2304]{1,0:T(8,128)(2,1)} %select_convert_fusion.2.qkv, f32[5,1536]{1,0:T(8,128)} %pad_maximum_fusion.1.taps, bf16[192,1536]{1,0:T(8,128)(2,1)} %get-tuple-element.194.pooled, ...), custom_call_target="tpu_custom_call" | custom-call | tf_op jit(solution)/shard_map/pallas_call | solution.py:428
  363.2 7.4 %convolution_convert_fusion.6.refs_0_ = bf16[848,768]{1,0:T(8,128)(2,1)} fusion(bf16[848,2304]{1,0:T(8,128)(2,1)} %get-tuple-element.248, bf16[768,768]{1,0:T(8,128)(2,1)} %bitcast.217, bf16[768,768]{1,0:T(8,128)(2,1)} %bitcast.223, bf16[768,768]{1,0:T(8,128)(2,1)} %bitcast.229), kind=kOutput, calls=%fused_computation.154 | convolution fusion | flops 3012292608 | bytes 8749056 | tf_op jit(solution)/shard_map/dot_general | solution.py:52
  370.6 20.4 %shard_map.275 = (f32[256,768]{1,0:T(8,128)}, f32[64,768]{1,0:T(8,128)}, bf16[256,768]{1,0:T(8,128)(2,1)}, bf16[256,768]{1,0:T(8,128)(2,1)}, bf16[16,768]{1,0:T(8,128)(2,1)}) custom-call(bf16[848,768]{1,0:T(8,128)(2,1)} %convolution_convert_fusion.6.refs_0_), custom_call_target="tpu_custom_call" | custom-call | tf_op jit(solution)/shard_map/pallas_call | solution.py:139
  391.7 1.8 fusion.255
  397.8 23.0 %conditional.3 = ((bf16[768,2304]{1,0:T(8,128)(2,1)}, bf16[768,768]{1,0:T(8,128)(2,1)}, bf16[768,3072]{1,0:T(8,128)(2,1)}, bf16[3072,768]{1,0:T(8,128)(2,1)})) conditional(s32[]{:T(128)} %convert_element_type.283, () %tuple.28, (bf16[848,768]{1,0:T(8,128)(2,1)}, bf16[848,768]{1,0:T(8,128)(2,1)}, bf16[848,2304]{1,0:T(8,128)(2,1)}, ...), branch_computations={%region_43.44_spmd, %region_44.45_spmd} | conditional | flops 11484659712 | bytes 65470728 | solution.py:1013
  397.8 11.8 %fusion.36 = bf16[768,2304]{1,0:T(8,128)(2,1)} fusion(bf16[848,2304]{1,0:T(8,128)(2,1)} %get-tuple-element.83, bf16[848,2304]{1,0:T(8,128)(2,1)} %get-tuple-element.82, bf16[848,768]{1,0:T(8,128)(2,1)} %get-tuple-element.81, bf16[848,768]{1,0:T(8,128)(2,1)} %get-tuple-element.80), kind=kOutput, calls=%fused_computation.37 | convolution fusion | flops 6024658944 | bytes 13959168 | tf_op jit(solution)/shard_map/cond/branch_1_fun/dot_general | solution.py:48
  409.7 1.9 convolution_convert_fusion.5
  412.2 4.3 convolution_convert_fusion.4
  416.5 4.3 convolution_convert_fusion.3
  420.8 170.5 %shard_map.276 = (bf16[768,2304]{1,0:T(8,128)(2,1)}, bf16[768,768]{1,0:T(8,128)(2,1)}, bf16[768,3072]{1,0:T(8,128)(2,1)}, bf16[3072,768]{1,0:T(8,128)(2,1)}, f32[16,768]{1,0:T(8,128)}) custom-call(bf16[768,2304]{1,0:T(8,128)(2,1)} %get-tuple-element.251.refs_0_, bf16[768,768]{1,0:T(8,128)(2,1)} %get-tuple-element.252.refs_1_, ...), custom_call_target="tpu_custom_call" | custom-call | tf_op jit(solution)/shard_map/pallas_call | solution.py:846
  593.4 1.8 fusion.196
  595.2 2.6 select_convert_fusion.3
  597.8 3.2 slice_bitcast_fusion
  602.3 1.6 bitcast_convert_fusion.2
  603.9 7.5 %bitcast_convert_fusion.1 = f32[1,768,3072]{2,1,0:T(8,128)} fusion(bf16[768,3072]{1,0:T(8,128)(2,1)} %get-tuple-element.260, bf16[768,3072]{1,0:T(8,128)(2,1)S(1)} %bitcast.180, pred[]{:T(512)S(6)} %eq.24), kind=kLoop, calls=%fused_computation.73 | loop fusion | flops 4718592 | bytes 18874368 | tf_op jit(solution)/shard_map/broadcast_in_dim | solution.py:1052
  611.5 4.4 bitcast_convert_fusion
  (418 shorter events, 44.6 us)
Async XLA Ops:
  0.6 59.4 %copy-start = (bf16[1,768,768]{2,1,0:T(8,128)(2,1)S(1)}, bf16[1,768,768]{2,1,0:T(8,128)(2,1)}, u32[]{:S(2)}) copy-start(bf16[1,768,768]{2,1,0:T(8,128)(2,1)} %param.27) | copy-start | bytes 3538948
  0.7 27.2 %copy-start.116 = (f32[1,768]{1,0:T(1,128)S(1)}, f32[1,768]{1,0:T(1,128)}, u32[]{:S(2)}) copy-start(f32[1,768]{1,0:T(1,128)} %param.35) | copy-start | bytes 9220
  0.7 27.2 %copy-start.117 = (f32[1,768]{1,0:T(1,128)S(1)}, f32[1,768]{1,0:T(1,128)}, u32[]{:S(2)}) copy-start(f32[1,768]{1,0:T(1,128)} %param.34) | copy-start | bytes 9220
  0.7 27.3 %copy-start.94 = (f32[1,5,768]{2,0,1:T(1,128)S(1)}, f32[1,5,768]{2,0,1:T(1,128)}, u32[]{:S(2)}) copy-start(f32[1,5,768]{2,0,1:T(1,128)} %param.31) | copy-start | bytes 46084
  0.7 27.3 %copy-start.95 = (f32[1,5,768]{2,0,1:T(1,128)S(1)}, f32[1,5,768]{2,0,1:T(1,128)}, u32[]{:S(2)}) copy-start(f32[1,5,768]{2,0,1:T(1,128)} %param.30) | copy-start | bytes 46084
  2.9 54.1 %copy-start.69 = (s32[1,64]{1,0:T(1,128)}, s32[1,64]{1,0:T(1,128)S(1)}, u32[]{:S(2)}) copy-start(s32[1,64]{1,0:T(1,128)S(1)} %get-tuple-element.348) | copy-start | bytes 772
  2.9 54.1 %copy-start.73 = (s32[1,64]{1,0:T(1,128)}, s32[1,64]{1,0:T(1,128)S(1)}, u32[]{:S(2)}) copy-start(s32[1,64]{1,0:T(1,128)S(1)} %get-tuple-element.350) | copy-start | bytes 772
  2.9 54.8 %copy-start.71 = (s32[1,64]{1,0:T(1,128)}, s32[1,64]{1,0:T(1,128)S(1)}, u32[]{:S(2)}) copy-start(s32[1,64]{1,0:T(1,128)S(1)} %get-tuple-element.349) | copy-start | bytes 772
  3.6 54.1 %copy-start.96 = (pred[64]{0:T(512)(128)(4,1)}, pred[64]{0:T(512)(128)(4,1)S(1)}, u32[]{:S(2)}) copy-start(pred[64]{0:T(512)(128)(4,1)S(1)} %iota_compare_fusion.3) | copy-start | bytes 196
  23.7 8.7 %copy-start.63 = (f32[768]{0:T(1024)}, f32[768]{0:T(1024)S(1)}, u32[]{:S(2)}) copy-start(f32[768]{0:T(1024)S(1)} %reduce.1) | copy-start | bytes 9220
  29.9 27.1 %copy-start.80 = (pred[64]{0:T(512)(128)(4,1)}, pred[64]{0:T(512)(128)(4,1)S(1)}, u32[]{:S(2)}) copy-start(pred[64]{0:T(512)(128)(4,1)S(1)} %get-tuple-element.376) | copy-start | bytes 196
  29.9 41.2 %copy-start.77 = (pred[64]{0:T(512)(128)(4,1)}, pred[64]{0:T(512)(128)(4,1)S(1)}, u32[]{:S(2)}) copy-start(pred[64]{0:T(512)(128)(4,1)S(1)} %get-tuple-element.377) | copy-start | bytes 196
  30.5 9.2 %copy-start.45 = (bf16[848,768]{1,0:T(8,128)(2,1)}, bf16[848,768]{1,0:T(8,128)(2,1)S(1)}, u32[]{:S(2)}) copy-start(bf16[848,768]{1,0:T(8,128)(2,1)S(1)} %fusion.138) | copy-start | bytes 3907588
  39.6 20.4 %copy-start.5 = (bf16[256,768]{1,0:T(8,128)(2,1)S(1)}, bf16[256,768]{1,0:T(8,128)(2,1)}, u32[]{:S(2)}) copy-start(bf16[256,768]{1,0:T(8,128)(2,1)} %copy-done.4) | copy-start | bytes 1179652
  68.6 28.2 %copy-start.55 = (bf16[256,768]{1,0:T(8,128)(2,1)}, bf16[256,768]{1,0:T(8,128)(2,1)S(1)}, u32[]{:S(2)}) copy-start(bf16[256,768]{1,0:T(8,128)(2,1)S(1)} %fusion.154) | copy-start | bytes 1179652
  68.6 1.8 collective-permute-start
  72.0 24.8 %copy-start.127 = (pred[848]{0:T(1024)(128)(4,1)S(1)}, pred[848]{0:T(1024)(128)(4,1)}, u32[]{:S(2)}) copy-start(pred[848]{0:T(1024)(128)(4,1)} %copy-done.126) | copy-start | bytes 2548
  102.2 20.2 %copy-start.75 = (s32[1,64]{1,0:T(1,128)S(1)}, s32[1,64]{1,0:T(1,128)}, u32[]{:S(2)}) copy-start(s32[1,64]{1,0:T(1,128)} %copy-done.73) | copy-start | bytes 772
  102.2 20.2 %copy-start.78 = (pred[64]{0:T(512)(128)(4,1)S(1)}, pred[64]{0:T(512)(128)(4,1)}, u32[]{:S(2)}) copy-start(pred[64]{0:T(512)(128)(4,1)} %copy-done.77) | copy-start | bytes 196
  102.2 20.2 %copy-start.119 = (pred[256]{0:T(512)(128)(4,1)S(1)}, pred[256]{0:T(512)(128)(4,1)}, u32[]{:S(2)}) copy-start(pred[256]{0:T(512)(128)(4,1)} %get-tuple-element.319) | copy-start | bytes 772
  102.2 21.9 %copy-start.7 = (bf16[256,768]{1,0:T(8,128)(2,1)S(1)}, bf16[256,768]{1,0:T(8,128)(2,1)}, u32[]{:S(2)}) copy-start(bf16[256,768]{1,0:T(8,128)(2,1)} %copy-done.6) | copy-start | bytes 1179652
  134.2 2.7 collective-permute-start.1
  136.9 8.9 %copy-start.64 = (f32[768]{0:T(1024)S(1)}, f32[768]{0:T(1024)}, u32[]{:S(2)}) copy-start(f32[768]{0:T(1024)} %copy-done.63) | copy-start | bytes 9220
  139.3 8.2 %copy-start.128 = (pred[848]{0:T(1024)(128)(4,1)S(1)}, pred[848]{0:T(1024)(128)(4,1)}, u32[]{:S(2)}) copy-start(pred[848]{0:T(1024)(128)(4,1)} %copy-done.126) | copy-start | bytes 2548
  152.8 14.2 %copy-start.70 = (s32[1,64]{1,0:T(1,128)S(1)}, s32[1,64]{1,0:T(1,128)}, u32[]{:S(2)}) copy-start(s32[1,64]{1,0:T(1,128)} %copy-done.69) | copy-start | bytes 772
  152.8 14.2 %copy-start.81 = (pred[64]{0:T(512)(128)(4,1)S(1)}, pred[64]{0:T(512)(128)(4,1)}, u32[]{:S(2)}) copy-start(pred[64]{0:T(512)(128)(4,1)} %copy-done.80) | copy-start | bytes 196
  152.8 14.2 %copy-start.118 = (pred[256]{0:T(512)(128)(4,1)S(1)}, pred[256]{0:T(512)(128)(4,1)}, u32[]{:S(2)}) copy-start(pred[256]{0:T(512)(128)(4,1)} %get-tuple-element.318) | copy-start | bytes 772
  152.8 16.6 %copy-start.9 = (bf16[256,768]{1,0:T(8,128)(2,1)S(1)}, bf16[256,768]{1,0:T(8,128)(2,1)}, u32[]{:S(2)}) copy-start(bf16[256,768]{1,0:T(8,128)(2,1)} %copy-done.8) | copy-start | bytes 1179652
  169.4 9.1 %slice-start.12 = ((s8[4718592]{0:T(1024)(128)(4,1)}), s8[4194304]{0:T(1024)(128)(4,1)S(1)}, s32[]{:S(2)}) async-start(s8[4718592]{0:T(1024)(128)(4,1)} %bitcast.210), calls=%async_computation.12 | async-start | bytes 8388608
  170.0 10.8 %copy-start.12 = (f32[256,768]{1,0:T(8,128)}, f32[256,768]{1,0:T(8,128)S(1)}, u32[]{:S(2)}) copy-start(f32[256,768]{1,0:T(8,128)S(1)} %get-tuple-element.363) | copy-start | bytes 2359300
  213.1 31.2 %copy-start.111 = (f32[256]{0:T(256)S(1)}, f32[256]{0:T(256)}, u32[]{:S(2)}) copy-start(f32[256]{0:T(256)} %get-tuple-element.321) | copy-start | bytes 3076
  213.1 31.7 %copy-start.112 = (f32[256]{0:T(256)S(1)}, f32[256]{0:T(256)}, u32[]{:S(2)}) copy-start(f32[256]{0:T(256)} %get-tuple-element.325) | copy-start | bytes 3076
  213.1 32.6 %copy-start.129 = (f32[256,3072]{1,0:T(8,128)S(1)}, f32[256,3072]{1,0:T(8,128)}, u32[]{:S(2)}) copy-start(f32[256,3072]{1,0:T(8,128)} %get-tuple-element.361) | copy-start | bytes 9437188
  216.7 33.4 %slice-start.14 = ((s8[4718592]{0:T(1024)(128)(4,1)}), s8[4194304]{0:T(1024)(128)(4,1)S(1)}, s32[]{:S(2)}) async-start(s8[4718592]{0:T(1024)(128)(4,1)} %bitcast.212), calls=%async_computation.14 | async-start | bytes 8388608
  217.1 28.6 %copy-start.36 = (bf16[256,768]{1,0:T(8,128)(2,1)}, bf16[256,768]{1,0:T(8,128)(2,1)S(1)}, u32[]{:S(2)}) copy-start(bf16[256,768]{1,0:T(8,128)(2,1)S(1)} %add_convert_fusion.2) | copy-start | bytes 1179652
  217.1 28.5 %collective-permute-start.2 = (bf16[256,768]{1,0:T(8,128)(2,1)S(1)}, bf16[256,768]{1,0:T(8,128)(2,1)S(1)}, u32[]{:S(2)}, u32[]{:S(2)}) collective-permute-start(bf16[256,768]{1,0:T(8,128)(2,1)S(1)} %add_convert_fusion.2), channel_id=1, source_target_pairs={{0,16},{16,0},{1,17},{17,1},{2,18},{18,2},{3,19},{19,3},{4,20},{20... | collective-permute-start | bytes 1179656 | tf_op jit(solution)/shard_map/ppermute | solution.py:939
  251.8 65.3 %copy-start.92 = (f32[768]{0:T(1024)}, f32[768]{0:T(1024)S(1)}, u32[]{:S(2)}) copy-start(f32[768]{0:T(1024)S(1)} %get-tuple-element.239) | copy-start | bytes 9220
  251.8 65.9 %copy-start.90 = (f32[768]{0:T(1024)}, f32[768]{0:T(1024)S(1)}, u32[]{:S(2)}) copy-start(f32[768]{0:T(1024)S(1)} %get-tuple-element.241) | copy-start | bytes 9220
  308.8 6.3 %collective-permute-start.3 = (bf16[256,768]{1,0:T(8,128)(2,1)S(1)}, bf16[256,768]{1,0:T(8,128)(2,1)S(1)}, u32[]{:S(2)}, u32[]{:S(2)}) collective-permute-start(bf16[256,768]{1,0:T(8,128)(2,1)S(1)} %add_convert_fusion.1), channel_id=1, source_target_pairs={{0,16},{16,0},{1,17},{17,1},{2,18},{18,2},{3,19},{19,3},{4,20},{20... | collective-permute-start | bytes 1179656 | tf_op jit(solution)/shard_map/ppermute | solution.py:939
  309.0 8.7 %copy-start.114 = (f32[768]{0:T(1024)S(1)}, f32[768]{0:T(1024)}, u32[]{:S(2)}) copy-start(f32[768]{0:T(1024)} %get-tuple-element.240) | copy-start | bytes 9220
  309.0 9.3 %copy-start.62 = (f32[5,1536]{1,0:T(8,128)S(1)}, f32[5,1536]{1,0:T(8,128)}, u32[]{:S(2)}) copy-start(f32[5,1536]{1,0:T(8,128)} %get-tuple-element.233) | copy-start | bytes 92164
  309.0 9.3 %copy-start.65 = (f32[5,1536]{1,0:T(8,128)S(1)}, f32[5,1536]{1,0:T(8,128)}, u32[]{:S(2)}) copy-start(f32[5,1536]{1,0:T(8,128)} %get-tuple-element.232) | copy-start | bytes 92164
  309.0 9.9 %copy-start.30 = (bf16[256,768]{1,0:T(8,128)(2,1)S(1)}, bf16[256,768]{1,0:T(8,128)(2,1)}, u32[]{:S(2)}) copy-start(bf16[256,768]{1,0:T(8,128)(2,1)} %copy-done.29) | copy-start | bytes 1179652
  309.0 9.9 %copy-start.35 = (bf16[256,768]{1,0:T(8,128)(2,1)S(1)}, bf16[256,768]{1,0:T(8,128)(2,1)}, u32[]{:S(2)}) copy-start(bf16[256,768]{1,0:T(8,128)(2,1)} %copy-done.34) | copy-start | bytes 1179652
  309.0 9.9 %copy-start.39 = (bf16[256,768]{1,0:T(8,128)(2,1)S(1)}, bf16[256,768]{1,0:T(8,128)(2,1)}, u32[]{:S(2)}) copy-start(bf16[256,768]{1,0:T(8,128)(2,1)} %copy-done.38) | copy-start | bytes 1179652
  326.6 71.2 %copy-start.21 = (bf16[256,768]{1,0:T(8,128)(2,1)}, bf16[256,768]{1,0:T(8,128)(2,1)S(1)}, u32[]{:S(2)}) copy-start(bf16[256,768]{1,0:T(8,128)(2,1)S(1)} %bitcast_select_fusion) | copy-start | bytes 1179652
  338.0 25.1 %copy-start.102 = (f32[256]{0:T(256)}, f32[256]{0:T(256)S(1)}, u32[]{:S(2)}) copy-start(f32[256]{0:T(256)S(1)} %negate_multiply_fusion.1) | copy-start | bytes 3076
  339.1 24.1 %copy-start.43 = (bf16[256,768]{1,0:T(8,128)(2,1)}, bf16[256,768]{1,0:T(8,128)(2,1)S(1)}, u32[]{:S(2)}) copy-start(bf16[256,768]{1,0:T(8,128)(2,1)S(1)} %fusion.195) | copy-start | bytes 1179652
  363.2 27.8 %copy-start.66 = (f32[5,1536]{1,0:T(8,128)S(1)}, f32[5,1536]{1,0:T(8,128)}, u32[]{:S(2)}) copy-start(f32[5,1536]{1,0:T(8,128)} %get-tuple-element.255) | copy-start | bytes 92164
  363.2 28.5 %copy-start.82 = (f32[256]{0:T(256)S(1)}, f32[256]{0:T(256)}, u32[]{:S(2)}) copy-start(f32[256]{0:T(256)} %broadcast_multiply_fusion.3) | copy-start | bytes 3076
  370.6 24.8 %copy-start.68 = (f32[768]{0:T(1024)S(1)}, f32[768]{0:T(1024)}, u32[]{:S(2)}) copy-start(f32[768]{0:T(1024)} %copy-done.67) | copy-start | bytes 9220
  370.6 26.0 %copy-start.93 = (f32[768]{0:T(1024)S(1)}, f32[768]{0:T(1024)}, u32[]{:S(2)}) copy-start(f32[768]{0:T(1024)} %copy-done.92) | copy-start | bytes 9220
  370.6 26.6 %copy-start.91 = (f32[768]{0:T(1024)S(1)}, f32[768]{0:T(1024)}, u32[]{:S(2)}) copy-start(f32[768]{0:T(1024)} %copy-done.90) | copy-start | bytes 9220
  370.6 26.6 %copy-start.28 = (bf16[256,768]{1,0:T(8,128)(2,1)S(1)}, bf16[256,768]{1,0:T(8,128)(2,1)}, u32[]{:S(2)}) copy-start(bf16[256,768]{1,0:T(8,128)(2,1)} %copy-done.27) | copy-start | bytes 1179652
  370.6 26.6 %copy-start.31 = (bf16[256,768]{1,0:T(8,128)(2,1)S(1)}, bf16[256,768]{1,0:T(8,128)(2,1)}, u32[]{:S(2)}) copy-start(bf16[256,768]{1,0:T(8,128)(2,1)} %copy-done.29) | copy-start | bytes 1179652
  397.8 11.9 %copy-start.40 = (bf16[256,768]{1,0:T(8,128)(2,1)S(1)}, bf16[256,768]{1,0:T(8,128)(2,1)}, u32[]{:S(2)}) copy-start(bf16[256,768]{1,0:T(8,128)(2,1)} %get-tuple-element.86) | copy-start | bytes 1179652 | tf_op jit(solution)/shard_map/cond
  397.8 11.9 %copy-start.44 = (bf16[256,768]{1,0:T(8,128)(2,1)S(1)}, bf16[256,768]{1,0:T(8,128)(2,1)}, u32[]{:S(2)}) copy-start(bf16[256,768]{1,0:T(8,128)(2,1)} %get-tuple-element.87) | copy-start | bytes 1179652 | tf_op jit(solution)/shard_map/cond
  420.8 172.6 %copy-start.22 = (bf16[256,768]{1,0:T(8,128)(2,1)S(1)}, bf16[256,768]{1,0:T(8,128)(2,1)}, u32[]{:S(2)}) copy-start(bf16[256,768]{1,0:T(8,128)(2,1)} %copy-done.21) | copy-start | bytes 1179652
  420.8 172.6 %copy-start.83 = (f32[256]{0:T(256)S(1)}, f32[256]{0:T(256)}, u32[]{:S(2)}) copy-start(f32[256]{0:T(256)} %broadcast_multiply_fusion.3) | copy-start | bytes 3076
  420.8 172.6 %copy-start.99 = (f32[256]{0:T(256)S(1)}, f32[256]{0:T(256)}, u32[]{:S(2)}) copy-start(f32[256]{0:T(256)} %copy-done.98) | copy-start | bytes 3076
  420.8 172.6 %copy-start.101 = (f32[256]{0:T(256)S(1)}, f32[256]{0:T(256)}, u32[]{:S(2)}) copy-start(f32[256]{0:T(256)} %copy-done.100) | copy-start | bytes 3076
  595.2 8.7 %slice-start.2 = ((s8[4718592]{0:T(1024)(128)(4,1)}), s8[4194304]{0:T(1024)(128)(4,1)S(1)}, s32[]{:S(2)}) async-start(s8[4718592]{0:T(1024)(128)(4,1)} %bitcast.179), calls=%async_computation.2 | async-start | bytes 8388608
  602.3 9.1 %slice-start = ((s8[4718592]{0:T(1024)(128)(4,1)}), s8[4194304]{0:T(1024)(128)(4,1)S(1)}, s32[]{:S(2)}) async-start(s8[4718592]{0:T(1024)(128)(4,1)} %bitcast.177), calls=%async_computation | async-start | bytes 8388608
  602.3 9.1 %slice-start.4 = ((s8[4718592]{0:T(1024)(128)(4,1)}), s8[4194304]{0:T(1024)(128)(4,1)S(1)}, s32[]{:S(2)}) async-start(s8[4718592]{0:T(1024)(128)(4,1)} %bitcast.181), calls=%async_computation.4 | async-start | bytes 8388608
  (92 other events, 371.6 us)

commit v2 on v1

--- a/solution.py
+++ b/solution.py
@@ -1038,26 +1038,28 @@
         section == 0, jnp.stack(back[1:][::-1]), jnp.stack(back[:micro][::-1])
     )
     reduce_section(0)
-    *sums, little = [
-        jnp.where(section == 0, mine, other).astype(full) for other, mine in zip(*reduced)
-    ]
     taps = key_pool.shape[1]
-    return (
-        produced[None],
-        back_grads[None],
-        sums[0][None, :, :width],
-        sums[0][None, :, width : 2 * width],
-        sums[0][None, :, 2 * width :],
-        sums[1][None],
-        sums[2][None],
-        sums[3][None],
-        little[None, :taps],
-        little[None, taps : 2 * taps],
-        little[2 * taps : 2 * taps + 1],
-        little[2 * taps + 1 : 2 * taps + 2],
-        little[2 * taps + 2 : 2 * taps + 3],
-        little[2 * taps + 3 : 2 * taps + 4],
+
+    def finished(parts):
+        *sums, little = [part.astype(full) for part in parts]
+        return (
+            sums[0][:, :width],
+            sums[0][:, width : 2 * width],
+            sums[0][:, 2 * width :],
+            sums[1],
+            sums[2],
+            sums[3],
+            little[:taps],
+            little[taps : 2 * taps],
+        ) + tuple(little[2 * taps + k] for k in range(4))
+
+    outs = lax.cond(
+        section == 0,
+        lambda early, late: finished(late),
+        lambda early, late: finished(early),
+        *reduced,
     )
+    return (produced[None], back_grads[None]) + tuple(out[None] for out in outs)
 
 
 def solution(mesh):

time: 626 us -> 610 us (0.974)
  other arithmetic: 57.4 us -> 41.6 us
    broadcast_in_dim x3, other arithmetic: 13.4 us -> 2.18 us  [per_device(): out[None]]
    unnamed x291 -> x211, local copies, waits for them, and re-layouts: 9.57 us -> 12.6 us
where the time goes in v2:
time: 610 us; the launch traced here: 602 us
  Pallas kernels  377 us (62%)
  matrix products  128 us (21%)
  other arithmetic  41.6 us (7%)
  starting transfers between devices  26.3 us (4%)
  local copies, waits for them, and re-layouts  24.1 us (4%)
    pallas_call x2, Pallas kernels, reduce_all(): pl.pallas_call(functools.partial(reduce_kernel, count, blocks, side, acro...  177 us
    pallas_call x6, Pallas kernels, vmem_call(): pl.pallas_call(kernel, out_shape=[jax.ShapeDtypeStruct(s, t) for s, t in...  116 us
    pallas_call x6, Pallas kernels, exchange(): pl.pallas_call(kernel, out_shape=[jax.ShapeDtypeStruct(s, t) for s, t in...  84.8 us
    dot_general x18, matrix products, mm(): return jnp.dot(left, right, preferred_element_type=full)  50.4 us
    dot_general x12, matrix products, nt(): lax.dot_general(left, right, (((1,), (1,)), ((), ())), preferred_element_...  44.3 us
    dot_general x10, matrix products, tn(): lax.dot_general(left, right, (((0,), (0,)), ((), ())), preferred_element_...  32.9 us
    ppermute x4, starting transfers between devices, to_partner(): return lax.ppermute(block, SECTION, [(0, 1), (1, 0)])  26.3 us
    unnamed x211, local copies, waits for them, and re-layouts  12.6 us
  transfers between devices with their start and end apart: 4, of which 2 were waited for; matrix products, arithmetic and copies ran while one was open for 2% of the time, Pallas kernels for 0%

profile of v2, /device:TPU:0, one launch (start us, length us, event | category | flops | bytes accessed | tf_op | source)
XLA Modules:
  0.0 602.3 jit_solution(15122042611329547380)
XLA Ops:
  0.7 1.4 fusion.263
  5.6 16.7 %shard_map.263 = bf16[848,768]{1,0:T(8,128)(2,1)} custom-call(bf16[256,768]{1,0:T(8,128)(2,1)} %copy-done.4, bf16[64,768]{1,0:T(8,128)(2,1)} %convolution_convert_fusion.17.refs_1_), custom_call_target="tpu_custom_call" | custom-call | tf_op jit(solution)/shard_map/pallas_call | solution.py:139
  23.9 1.6 convert_reduce_fusion.2
  25.4 1.8 fusion.135
  28.0 1.3 iota_compare_fusion.1
  29.9 1.9 pad_add_fusion
  31.8 7.2 %select_convert_fusion.2.qkv = bf16[848,2304]{1,0:T(8,128)(2,1)} fusion(bf16[848,768]{1,0:T(8,128)(2,1)S(1)} %fusion.138, pred[848]{0:T(1024)(128)(4,1)S(1)} %fusion.245, bf16[768,768]{1,0:T(8,128)(2,1)} %bitcast.235, bf16[768,768]{1,0:T(8,128)(2,1)} %bitcast.241, bf16[768,768]{1,0:T(8,128)(2,1)} %bitcast.247), kind=kOutput, calls=%fused_computation.84 | convolution fusion | flops 3015548928 | bytes 8749904 | tf_op jit(solution)/shard_map/dot_general | solution.py:44
  39.0 17.3 %shard_map.264 = (f32[256,768]{1,0:T(8,128)}, bf16[192,1536]{1,0:T(8,128)(2,1)}, f32[16,256]{1,0:T(8,128)}, f32[64,768]{1,0:T(8,128)}, f32[16,128]{1,0:T(8,128)}) custom-call(s32[4]{0:T(128)} %get-tuple-element.507.scalars, bf16[848,2304]{1,0:T(8,128)(2,1)} %select_convert_fusion.2.qkv, f32[5,1536]{1,0:T(8,128)} %pad_maximum_fusion.1.taps), custom_call_target="tpu_custom_call" | custom-call | tf_op jit(solution)/shard_map/pallas_call | solution.py:428
  56.5 1.6 fusion.157
  60.0 5.8 multiply_convert_fusion.2
  65.9 1.4 fusion.154
  67.4 1.7 collective-permute-done
  70.2 19.8 %shard_map.265 = bf16[848,768]{1,0:T(8,128)(2,1)} custom-call(bf16[256,768]{1,0:T(8,128)(2,1)} %copy-done.6, bf16[64,768]{1,0:T(8,128)(2,1)} %convolution_convert_fusion.16.refs_1_), custom_call_target="tpu_custom_call" | custom-call | tf_op jit(solution)/shard_map/pallas_call | solution.py:139
  90.1 1.7 convert_reduce_fusion.1
  91.8 1.9 fusion.131
  94.3 5.4 select_convert_fusion.1.qkv
  99.7 20.1 %shard_map.266 = (f32[256,768]{1,0:T(8,128)}, bf16[192,1536]{1,0:T(8,128)(2,1)}, f32[16,256]{1,0:T(8,128)}, f32[64,768]{1,0:T(8,128)}, f32[16,128]{1,0:T(8,128)}) custom-call(s32[4]{0:T(128)} %get-tuple-element.508.scalars, bf16[848,2304]{1,0:T(8,128)(2,1)} %select_convert_fusion.1.qkv, f32[5,1536]{1,0:T(8,128)} %pad_maximum_fusion.1.taps), custom_call_target="tpu_custom_call" | custom-call | tf_op jit(solution)/shard_map/pallas_call | solution.py:428
  119.8 1.6 fusion.158
  123.2 6.2 %multiply_convert_fusion.1 = (bf16[256,3072]{1,0:T(8,128)(2,1)S(1)}, f32[256,3072]{1,0:T(8,128)}) fusion(bf16[256,768]{1,0:T(8,128)(2,1)S(1)} %add_convert_fusion.4, bf16[1,768,3072]{2,1,0:T(8,128)(2,1)} %param.30), kind=kOutput, calls=%fused_computation.142 | convolution fusion | flops 1211891712 | bytes 9830400 | tf_op jit(solution)/shard_map/dot_general | solution.py:44
  129.5 2.2 fusion.151
  131.7 1.2 pad_add_fusion.3.scalars
  132.9 1.8 select_bitcast_fusion
  136.8 2.8 shard_map.267
  139.6 1.7 convert_reduce_fusion
  141.4 1.9 fusion.127
  145.0 5.3 select_convert_fusion.qkv
  150.3 14.1 %shard_map.268 = (f32[256,768]{1,0:T(8,128)}, bf16[192,1536]{1,0:T(8,128)(2,1)}, f32[16,256]{1,0:T(8,128)}, f32[64,768]{1,0:T(8,128)}, f32[16,128]{1,0:T(8,128)}) custom-call(s32[4]{0:T(128)} %pad_add_fusion.3.scalars, bf16[848,2304]{1,0:T(8,128)(2,1)} %select_convert_fusion.qkv, f32[5,1536]{1,0:T(8,128)} %pad_maximum_fusion.1.taps), custom_call_target="tpu_custom_call" | custom-call | tf_op jit(solution)/shard_map/pallas_call | solution.py:428
  164.5 1.6 fusion.159
  167.2 6.1 %multiply_convert_fusion = (bf16[256,3072]{1,0:T(8,128)(2,1)}, f32[256,3072]{1,0:T(8,128)S(1)}) fusion(bf16[256,768]{1,0:T(8,128)(2,1)S(1)} %add_convert_fusion.3, bf16[1,768,3072]{2,1,0:T(8,128)(2,1)} %param.30), kind=kOutput, calls=%fused_computation.140 | convolution fusion | flops 1211891712 | bytes 9830400 | tf_op jit(solution)/shard_map/dot_general | solution.py:44
  173.3 2.0 fusion.103
  175.4 1.7 multiply_reduce_fusion.3
  179.9 19.4 %shard_map.269 = (bf16[848,2304]{1,0:T(8,128)(2,1)}, f32[5,1536]{1,0:T(8,128)}) custom-call(s32[4]{0:T(128)} %pad_add_fusion.3.scalars, bf16[848,2304]{1,0:T(8,128)(2,1)} %select_convert_fusion.qkv, f32[5,1536]{1,0:T(8,128)} %pad_maximum_fusion.1.taps, bf16[192,1536]{1,0:T(8,128)(2,1)} %get-tuple-element.257.pooled, f32[16,256]{1,0:T(8,128)} %get-tuple-element.258.stats, ...), custom_call_target="tpu_custom_call" | custom-call | tf_op jit(solution)/shard_map/pallas_call | solution.py:428
  199.3 7.4 %convolution_convert_fusion.8.refs_0_ = bf16[848,768]{1,0:T(8,128)(2,1)} fusion(bf16[848,2304]{1,0:T(8,128)(2,1)} %get-tuple-element.271, bf16[768,768]{1,0:T(8,128)(2,1)} %bitcast.236, bf16[768,768]{1,0:T(8,128)(2,1)} %bitcast.242, bf16[768,768]{1,0:T(8,128)(2,1)} %bitcast.248), kind=kOutput, calls=%fused_computation.166 | convolution fusion | flops 3012292608 | bytes 8749056 | tf_op jit(solution)/shard_map/dot_general | solution.py:52
  206.7 2.9 shard_map.270
  209.6 2.0 fusion.257
  212.6 26.2 %collective-permute-start.2 = (bf16[256,768]{1,0:T(8,128)(2,1)S(1)}, bf16[256,768]{1,0:T(8,128)(2,1)S(1)}, u32[]{:S(2)}, u32[]{:S(2)}) collective-permute-start(bf16[256,768]{1,0:T(8,128)(2,1)S(1)} %add_convert_fusion.2), channel_id=1, source_target_pairs={{0,16},{16,0},{1,17},{17,1},{2,18},{18,2},{3,19},{19,3},{4,20},{20... | collective-permute-start | bytes 1179656 | tf_op jit(solution)/shard_map/ppermute | solution.py:939
  240.2 4.3 fusion.100
  244.6 1.7 multiply_reduce_fusion.2
  249.1 21.9 %shard_map.271 = (bf16[848,2304]{1,0:T(8,128)(2,1)}, f32[5,1536]{1,0:T(8,128)}) custom-call(s32[4]{0:T(128)} %get-tuple-element.508.scalars, bf16[848,2304]{1,0:T(8,128)(2,1)} %select_convert_fusion.1.qkv, f32[5,1536]{1,0:T(8,128)} %pad_maximum_fusion.1.taps, bf16[192,1536]{1,0:T(8,128)(2,1)} %get-tuple-element.254.pooled, ...), custom_call_target="tpu_custom_call" | custom-call | tf_op jit(solution)/shard_map/pallas_call | solution.py:428
  271.0 7.4 %convolution_convert_fusion.7.refs_0_ = bf16[848,768]{1,0:T(8,128)(2,1)} fusion(bf16[848,2304]{1,0:T(8,128)(2,1)} %get-tuple-element.272, bf16[768,768]{1,0:T(8,128)(2,1)} %bitcast.237, bf16[768,768]{1,0:T(8,128)(2,1)} %bitcast.243, bf16[768,768]{1,0:T(8,128)(2,1)} %bitcast.249), kind=kOutput, calls=%fused_computation.165 | convolution fusion | flops 3012292608 | bytes 8749056 | tf_op jit(solution)/shard_map/dot_general | solution.py:52
  278.5 21.9 %shard_map.272 = (f32[256,768]{1,0:T(8,128)}, f32[64,768]{1,0:T(8,128)}, bf16[256,768]{1,0:T(8,128)(2,1)}, bf16[256,768]{1,0:T(8,128)(2,1)}, bf16[16,768]{1,0:T(8,128)(2,1)}) custom-call(bf16[848,768]{1,0:T(8,128)(2,1)} %convolution_convert_fusion.7.refs_0_), custom_call_target="tpu_custom_call" | custom-call | tf_op jit(solution)/shard_map/pallas_call | solution.py:139
  300.4 2.0 fusion.256
  303.4 3.8 fusion.160
  307.3 2.1 maximum_select_fusion
  313.2 6.4 %shard_map.273 = (bf16[768,2304]{1,0:T(8,128)(2,1)}, bf16[768,768]{1,0:T(8,128)(2,1)}, bf16[768,3072]{1,0:T(8,128)(2,1)}, bf16[3072,768]{1,0:T(8,128)(2,1)}, f32[16,768]{1,0:T(8,128)}) custom-call(bf16[768,2304]{1,0:T(8,128)(2,1)} %get-tuple-element.285.refs_0_, bf16[768,768]{1,0:T(8,128)(2,1)} %get-tuple-element.286.refs_1_, ...), custom_call_target="tpu_custom_call" | custom-call | tf_op jit(solution)/shard_map/pallas_call | solution.py:846
  320.8 6.3 %fusion.97 = bf16[256,3072]{1,0:T(8,128)(2,1)S(1)} fusion(bf16[256,768]{1,0:T(8,128)(2,1)S(1)} %bitcast_select_fusion, bf16[1,3072,768]{2,1,0:T(8,128)(2,1)} %param.31, f32[256,3072]{1,0:T(8,128)} %get-tuple-element.492), kind=kOutput, calls=%fused_computation.115 | convolution fusion | flops 1217396736 | bytes 9830400 | tf_op jit(solution)/shard_map/dot_general | solution.py:52
  327.1 4.6 multiply_reduce_fusion
  334.5 22.7 %shard_map.274 = (bf16[848,2304]{1,0:T(8,128)(2,1)}, f32[5,1536]{1,0:T(8,128)}) custom-call(s32[4]{0:T(128)} %get-tuple-element.507.scalars, bf16[848,2304]{1,0:T(8,128)(2,1)} %select_convert_fusion.2.qkv, f32[5,1536]{1,0:T(8,128)} %pad_maximum_fusion.1.taps, bf16[192,1536]{1,0:T(8,128)(2,1)} %get-tuple-element.251.pooled, ...), custom_call_target="tpu_custom_call" | custom-call | tf_op jit(solution)/shard_map/pallas_call | solution.py:428
  357.1 7.4 %convolution_convert_fusion.6.refs_0_ = bf16[848,768]{1,0:T(8,128)(2,1)} fusion(bf16[848,2304]{1,0:T(8,128)(2,1)} %get-tuple-element.305, bf16[768,768]{1,0:T(8,128)(2,1)} %bitcast.238, bf16[768,768]{1,0:T(8,128)(2,1)} %bitcast.244, bf16[768,768]{1,0:T(8,128)(2,1)} %bitcast.250), kind=kOutput, calls=%fused_computation.164 | convolution fusion | flops 3012292608 | bytes 8749056 | tf_op jit(solution)/shard_map/dot_general | solution.py:52
  364.6 20.7 %shard_map.275 = (f32[256,768]{1,0:T(8,128)}, f32[64,768]{1,0:T(8,128)}, bf16[256,768]{1,0:T(8,128)(2,1)}, bf16[256,768]{1,0:T(8,128)(2,1)}, bf16[16,768]{1,0:T(8,128)(2,1)}) custom-call(bf16[848,768]{1,0:T(8,128)(2,1)} %convolution_convert_fusion.6.refs_0_), custom_call_target="tpu_custom_call" | custom-call | tf_op jit(solution)/shard_map/pallas_call | solution.py:139
  385.4 1.8 fusion.255
  391.8 23.0 %conditional.4 = ((bf16[768,2304]{1,0:T(8,128)(2,1)}, bf16[768,768]{1,0:T(8,128)(2,1)}, bf16[768,3072]{1,0:T(8,128)(2,1)}, bf16[3072,768]{1,0:T(8,128)(2,1)})) conditional(s32[]{:T(128)} %convert_element_type.294, () %tuple.45, (bf16[848,768]{1,0:T(8,128)(2,1)}, bf16[848,768]{1,0:T(8,128)(2,1)}, bf16[848,2304]{1,0:T(8,128)(2,1)}, ...), branch_computations={%region_43.44_spmd, %region_44.45_spmd} | conditional | flops 11484659712 | bytes 68616512 | solution.py:1013
  391.8 11.9 %fusion.36 = bf16[768,2304]{1,0:T(8,128)(2,1)} fusion(bf16[848,2304]{1,0:T(8,128)(2,1)} %get-tuple-element.135, bf16[848,2304]{1,0:T(8,128)(2,1)} %get-tuple-element.134, bf16[848,768]{1,0:T(8,128)(2,1)} %get-tuple-element.133, bf16[848,768]{1,0:T(8,128)(2,1)} %get-tuple-element.132), kind=kOutput, calls=%fused_computation.37 | convolution fusion | flops 6024658944 | bytes 13959168 | tf_op jit(solution)/shard_map/cond/branch_1_fun/dot_general | solution.py:48
  403.8 1.8 convolution_convert_fusion.5
  406.3 4.3 convolution_convert_fusion.4
  410.6 4.3 convolution_convert_fusion.3
  414.9 170.3 %shard_map.276 = (bf16[768,2304]{1,0:T(8,128)(2,1)}, bf16[768,768]{1,0:T(8,128)(2,1)}, bf16[768,3072]{1,0:T(8,128)(2,1)}, bf16[3072,768]{1,0:T(8,128)(2,1)}, f32[16,768]{1,0:T(8,128)S(1)}) custom-call(bf16[768,2304]{1,0:T(8,128)(2,1)} %get-tuple-element.313.refs_0_, bf16[768,768]{1,0:T(8,128)(2,1)} %get-tuple-element.314.refs_1_, ...), custom_call_target="tpu_custom_call" | custom-call | tf_op jit(solution)/shard_map/pallas_call | solution.py:846
  585.2 9.0 %conditional.5 = (f32[1,768,768]{2,1,0:T(8,128)}, f32[1,768,768]{2,1,0:T(8,128)}, f32[1,768,768]{2,1,0:T(8,128)}, f32[1,768,768]{2,1,0:T(8,128)S(1)}, f32[1,768,...) conditional(s32[]{:T(128)} %convert_element_type.294, ...), branch_computations={%region_49.50_spmd.clone, %region_50.51_spmd.clone} | conditional | flops 7077888 | bytes 89800928 | solution.py:1056
  585.2 2.7 convert_element_type.299
  587.9 3.1 slice_bitcast_fusion.5
  591.3 1.3 bitcast_convert_fusion.4
  594.4 1.2 maximum_select_fusion.1
  595.6 2.6 copy-done.16
  598.2 3.1 copy-done.17
  (353 shorter events, 40.7 us)
Async XLA Ops:
  0.6 58.3 %copy-start = (bf16[1,768,768]{2,1,0:T(8,128)(2,1)S(1)}, bf16[1,768,768]{2,1,0:T(8,128)(2,1)}, u32[]{:S(2)}) copy-start(bf16[1,768,768]{2,1,0:T(8,128)(2,1)} %param.29) | copy-start | bytes 3538948
  0.7 26.7 %copy-start.94 = (f32[1,768]{1,0:T(1,128)S(1)}, f32[1,768]{1,0:T(1,128)}, u32[]{:S(2)}) copy-start(f32[1,768]{1,0:T(1,128)} %param.37) | copy-start | bytes 9220
  0.7 26.7 %copy-start.95 = (f32[1,768]{1,0:T(1,128)S(1)}, f32[1,768]{1,0:T(1,128)}, u32[]{:S(2)}) copy-start(f32[1,768]{1,0:T(1,128)} %param.36) | copy-start | bytes 9220
  0.7 26.7 %copy-start.80 = (f32[1,5,768]{2,0,1:T(1,128)S(1)}, f32[1,5,768]{2,0,1:T(1,128)}, u32[]{:S(2)}) copy-start(f32[1,5,768]{2,0,1:T(1,128)} %param.33) | copy-start | bytes 46084
  0.7 26.7 %copy-start.81 = (f32[1,5,768]{2,0,1:T(1,128)S(1)}, f32[1,5,768]{2,0,1:T(1,128)}, u32[]{:S(2)}) copy-start(f32[1,5,768]{2,0,1:T(1,128)} %param.32) | copy-start | bytes 46084
  2.9 53.6 %copy-start.71 = (s32[1,64]{1,0:T(1,128)}, s32[1,64]{1,0:T(1,128)S(1)}, u32[]{:S(2)}) copy-start(s32[1,64]{1,0:T(1,128)S(1)} %get-tuple-element.484) | copy-start | bytes 772
  3.5 53.0 %copy-start.84 = (pred[64]{0:T(512)(128)(4,1)}, pred[64]{0:T(512)(128)(4,1)S(1)}, u32[]{:S(2)}) copy-start(pred[64]{0:T(512)(128)(4,1)S(1)} %iota_compare_fusion.3) | copy-start | bytes 196
  22.4 7.0 %copy-start.1 = (bf16[848,768]{1,0:T(8,128)(2,1)S(1)}, bf16[848,768]{1,0:T(8,128)(2,1)}, u32[]{:S(2)}) copy-start(bf16[848,768]{1,0:T(8,128)(2,1)} %shard_map.263) | copy-start | bytes 3907588
  29.9 9.1 %copy-start.48 = (bf16[848,768]{1,0:T(8,128)(2,1)}, bf16[848,768]{1,0:T(8,128)(2,1)S(1)}, u32[]{:S(2)}) copy-start(bf16[848,768]{1,0:T(8,128)(2,1)S(1)} %fusion.138) | copy-start | bytes 3907588
  39.0 19.9 %copy-start.5 = (bf16[256,768]{1,0:T(8,128)(2,1)S(1)}, bf16[256,768]{1,0:T(8,128)(2,1)}, u32[]{:S(2)}) copy-start(bf16[256,768]{1,0:T(8,128)(2,1)} %copy-done.4) | copy-start | bytes 1179652
  59.5 6.4 %copy-start.10 = (f32[256,768]{1,0:T(8,128)}, f32[256,768]{1,0:T(8,128)S(1)}, u32[]{:S(2)}) copy-start(f32[256,768]{1,0:T(8,128)S(1)} %get-tuple-element.490) | copy-start | bytes 2359300
  59.5 6.3 %copy-start.74 = (f32[256]{0:T(256)}, f32[256]{0:T(256)S(1)}, u32[]{:S(2)}) copy-start(f32[256]{0:T(256)S(1)} %broadcast_multiply_fusion.8) | copy-start | bytes 3076
  59.7 6.1 %copy-start.88 = (f32[256]{0:T(256)}, f32[256]{0:T(256)S(1)}, u32[]{:S(2)}) copy-start(f32[256]{0:T(256)S(1)} %multiply_reduce_fusion.8) | copy-start | bytes 3076
  59.7 6.1 %copy-start.86 = (f32[256]{0:T(256)}, f32[256]{0:T(256)S(1)}, u32[]{:S(2)}) copy-start(f32[256]{0:T(256)S(1)} %fusion.246) | copy-start | bytes 3076
  59.7 6.1 %slice-start.8 = ((s8[4718592]{0:T(1024)(128)(4,1)}), s8[4194304]{0:T(1024)(128)(4,1)S(1)}, s32[]{:S(2)}) async-start(s8[4718592]{0:T(1024)(128)(4,1)} %bitcast.225), calls=%async_computation.8 | async-start | bytes 8388608
  67.3 1.8 collective-permute-start
  99.7 22.5 %copy-start.7 = (bf16[256,768]{1,0:T(8,128)(2,1)S(1)}, bf16[256,768]{1,0:T(8,128)(2,1)}, u32[]{:S(2)}) copy-start(bf16[256,768]{1,0:T(8,128)(2,1)} %copy-done.6) | copy-start | bytes 1179652
  122.7 6.7 %copy-start.14 = (f32[256,768]{1,0:T(8,128)}, f32[256,768]{1,0:T(8,128)S(1)}, u32[]{:S(2)}) copy-start(f32[256,768]{1,0:T(8,128)S(1)} %get-tuple-element.494) | copy-start | bytes 2359300
  122.8 6.7 %slice-start.10 = ((s8[4718592]{0:T(1024)(128)(4,1)}), s8[4194304]{0:T(1024)(128)(4,1)S(1)}, s32[]{:S(2)}) async-start(s8[4718592]{0:T(1024)(128)(4,1)} %bitcast.227), calls=%async_computation.10 | async-start | bytes 8388608
  123.2 6.2 %copy-start.55 = (bf16[256,768]{1,0:T(8,128)(2,1)}, bf16[256,768]{1,0:T(8,128)(2,1)S(1)}, u32[]{:S(2)}) copy-start(bf16[256,768]{1,0:T(8,128)(2,1)S(1)} %add_convert_fusion.4) | copy-start | bytes 1179652
  123.2 6.2 %slice-start.11 = ((s8[4718592]{0:T(1024)(128)(4,1)}), s8[524288]{0:T(1024)(128)(4,1)S(1)}, s32[]{:S(2)}) async-start(s8[4718592]{0:T(1024)(128)(4,1)} %bitcast.227), calls=%async_computation.11 | async-start | bytes 1048576
  131.6 3.0 collective-permute-start.1
  150.3 15.8 %copy-start.9 = (bf16[256,768]{1,0:T(8,128)(2,1)S(1)}, bf16[256,768]{1,0:T(8,128)(2,1)}, u32[]{:S(2)}) copy-start(bf16[256,768]{1,0:T(8,128)(2,1)} %copy-done.8) | copy-start | bytes 1179652
  166.1 7.2 %copy-start.36 = (bf16[256,768]{1,0:T(8,128)(2,1)}, bf16[256,768]{1,0:T(8,128)(2,1)S(1)}, u32[]{:S(2)}) copy-start(bf16[256,768]{1,0:T(8,128)(2,1)S(1)} %fusion.159) | copy-start | bytes 1179652
  166.1 9.2 %slice-start.14 = ((s8[4718592]{0:T(1024)(128)(4,1)}), s8[4194304]{0:T(1024)(128)(4,1)S(1)}, s32[]{:S(2)}) async-start(s8[4718592]{0:T(1024)(128)(4,1)} %bitcast.231), calls=%async_computation.14 | async-start | bytes 8388608
  166.7 10.4 %copy-start.12 = (f32[256,768]{1,0:T(8,128)}, f32[256,768]{1,0:T(8,128)S(1)}, u32[]{:S(2)}) copy-start(f32[256,768]{1,0:T(8,128)S(1)} %get-tuple-element.498) | copy-start | bytes 2359300
  166.7 6.6 %slice-start.12 = ((s8[4718592]{0:T(1024)(128)(4,1)}), s8[4194304]{0:T(1024)(128)(4,1)S(1)}, s32[]{:S(2)}) async-start(s8[4718592]{0:T(1024)(128)(4,1)} %bitcast.229), calls=%async_computation.12 | async-start | bytes 8388608
  167.2 6.1 %copy-start.62 = (bf16[256,768]{1,0:T(8,128)(2,1)}, bf16[256,768]{1,0:T(8,128)(2,1)S(1)}, u32[]{:S(2)}) copy-start(bf16[256,768]{1,0:T(8,128)(2,1)S(1)} %add_convert_fusion.3) | copy-start | bytes 1179652
  167.2 6.1 %copy-start.60 = (bf16[256,768]{1,0:T(8,128)(2,1)S(1)}, bf16[256,768]{1,0:T(8,128)(2,1)}, u32[]{:S(2)}) copy-start(bf16[256,768]{1,0:T(8,128)(2,1)} %select_bitcast_fusion) | copy-start | bytes 1179652
  167.2 6.1 %slice-start.13 = ((s8[4718592]{0:T(1024)(128)(4,1)}), s8[524288]{0:T(1024)(128)(4,1)S(1)}, s32[]{:S(2)}) async-start(s8[4718592]{0:T(1024)(128)(4,1)} %bitcast.229), calls=%async_computation.13 | async-start | bytes 1048576
  167.2 8.2 %slice-start.15 = ((s8[4718592]{0:T(1024)(128)(4,1)}), s8[524288]{0:T(1024)(128)(4,1)S(1)}, s32[]{:S(2)}) async-start(s8[4718592]{0:T(1024)(128)(4,1)} %bitcast.231), calls=%async_computation.15 | async-start | bytes 1048576
  178.5 20.8 %copy-start.44 = (bf16[256,768]{1,0:T(8,128)(2,1)}, bf16[256,768]{1,0:T(8,128)(2,1)S(1)}, u32[]{:S(2)}) copy-start(bf16[256,768]{1,0:T(8,128)(2,1)S(1)} %fusion.193) | copy-start | bytes 1179652
  209.6 30.5 %copy-start.102 = (f32[256,3072]{1,0:T(8,128)S(1)}, f32[256,3072]{1,0:T(8,128)}, u32[]{:S(2)}) copy-start(f32[256,3072]{1,0:T(8,128)} %get-tuple-element.496) | copy-start | bytes 9437188
  212.1 32.4 %slice-start.16 = ((s8[4718592]{0:T(1024)(128)(4,1)}), s8[4194304]{0:T(1024)(128)(4,1)S(1)}, s32[]{:S(2)}) async-start(s8[4718592]{0:T(1024)(128)(4,1)} %bitcast.233), calls=%async_computation.16 | async-start | bytes 8388608
  212.5 27.6 %copy-start.39 = (bf16[256,768]{1,0:T(8,128)(2,1)}, bf16[256,768]{1,0:T(8,128)(2,1)S(1)}, u32[]{:S(2)}) copy-start(bf16[256,768]{1,0:T(8,128)(2,1)S(1)} %add_convert_fusion.2) | copy-start | bytes 1179652
  212.6 27.5 %collective-permute-start.2 = (bf16[256,768]{1,0:T(8,128)(2,1)S(1)}, bf16[256,768]{1,0:T(8,128)(2,1)S(1)}, u32[]{:S(2)}, u32[]{:S(2)}) collective-permute-start(bf16[256,768]{1,0:T(8,128)(2,1)S(1)} %add_convert_fusion.2), channel_id=1, source_target_pairs={{0,16},{16,0},{1,17},{17,1},{2,18},{18,2},{3,19},{19,3},{4,20},{20... | collective-permute-start | bytes 1179656 | tf_op jit(solution)/shard_map/ppermute | solution.py:939
  246.2 65.1 %copy-start.78 = (f32[768]{0:T(1024)}, f32[768]{0:T(1024)S(1)}, u32[]{:S(2)}) copy-start(f32[768]{0:T(1024)S(1)} %get-tuple-element.296) | copy-start | bytes 9220
  246.3 65.7 %copy-start.76 = (f32[768]{0:T(1024)}, f32[768]{0:T(1024)S(1)}, u32[]{:S(2)}) copy-start(f32[768]{0:T(1024)S(1)} %get-tuple-element.298) | copy-start | bytes 9220
  247.7 23.4 %copy-start.41 = (bf16[256,768]{1,0:T(8,128)(2,1)}, bf16[256,768]{1,0:T(8,128)(2,1)S(1)}, u32[]{:S(2)}) copy-start(bf16[256,768]{1,0:T(8,128)(2,1)S(1)} %fusion.194) | copy-start | bytes 1179652
  302.8 7.4 %copy-start.69 = (f32[768]{0:T(1024)}, f32[768]{0:T(1024)S(1)}, u32[]{:S(2)}) copy-start(f32[768]{0:T(1024)S(1)} %get-tuple-element.292) | copy-start | bytes 9220
  303.3 6.1 %collective-permute-start.3 = (bf16[256,768]{1,0:T(8,128)(2,1)S(1)}, bf16[256,768]{1,0:T(8,128)(2,1)S(1)}, u32[]{:S(2)}, u32[]{:S(2)}) collective-permute-start(bf16[256,768]{1,0:T(8,128)(2,1)S(1)} %add_convert_fusion.1), channel_id=1, source_target_pairs={{0,16},{16,0},{1,17},{17,1},{2,18},{18,2},{3,19},{19,3},{4,20},{20... | collective-permute-start | bytes 1179656 | tf_op jit(solution)/shard_map/ppermute | solution.py:939
  303.4 9.1 %copy-start.65 = (f32[5,1536]{1,0:T(8,128)S(1)}, f32[5,1536]{1,0:T(8,128)}, u32[]{:S(2)}) copy-start(f32[5,1536]{1,0:T(8,128)} %get-tuple-element.290) | copy-start | bytes 92164
  303.4 9.1 %copy-start.67 = (f32[5,1536]{1,0:T(8,128)S(1)}, f32[5,1536]{1,0:T(8,128)}, u32[]{:S(2)}) copy-start(f32[5,1536]{1,0:T(8,128)} %get-tuple-element.289) | copy-start | bytes 92164
  303.4 9.8 %copy-start.32 = (bf16[256,768]{1,0:T(8,128)(2,1)S(1)}, bf16[256,768]{1,0:T(8,128)(2,1)}, u32[]{:S(2)}) copy-start(bf16[256,768]{1,0:T(8,128)(2,1)} %copy-done.31) | copy-start | bytes 1179652
  320.8 6.3 %copy-start.11 = (f32[256,768]{1,0:T(8,128)S(1)}, f32[256,768]{1,0:T(8,128)}, u32[]{:S(2)}) copy-start(f32[256,768]{1,0:T(8,128)} %copy-done.10) | copy-start | bytes 2359300
  320.8 6.3 %copy-start.75 = (f32[256]{0:T(256)S(1)}, f32[256]{0:T(256)}, u32[]{:S(2)}) copy-start(f32[256]{0:T(256)} %copy-done.74) | copy-start | bytes 3076
  320.8 6.3 %copy-start.87 = (f32[256]{0:T(256)S(1)}, f32[256]{0:T(256)}, u32[]{:S(2)}) copy-start(f32[256]{0:T(256)} %copy-done.86) | copy-start | bytes 3076
  357.1 28.2 %copy-start.73 = (f32[256]{0:T(256)S(1)}, f32[256]{0:T(256)}, u32[]{:S(2)}) copy-start(f32[256]{0:T(256)} %broadcast_multiply_fusion.3) | copy-start | bytes 3076
  391.8 11.9 %copy-start.30 = (bf16[256,768]{1,0:T(8,128)(2,1)S(1)}, bf16[256,768]{1,0:T(8,128)(2,1)}, u32[]{:S(2)}) copy-start(bf16[256,768]{1,0:T(8,128)(2,1)} %get-tuple-element.137) | copy-start | bytes 1179652 | tf_op jit(solution)/shard_map/cond
  391.8 11.9 %copy-start.33 = (bf16[256,768]{1,0:T(8,128)(2,1)S(1)}, bf16[256,768]{1,0:T(8,128)(2,1)}, u32[]{:S(2)}) copy-start(bf16[256,768]{1,0:T(8,128)(2,1)} %get-tuple-element.136) | copy-start | bytes 1179652 | tf_op jit(solution)/shard_map/cond
  391.8 11.9 %copy-start.43 = (bf16[256,768]{1,0:T(8,128)(2,1)S(1)}, bf16[256,768]{1,0:T(8,128)(2,1)}, u32[]{:S(2)}) copy-start(bf16[256,768]{1,0:T(8,128)(2,1)} %get-tuple-element.138) | copy-start | bytes 1179652 | tf_op jit(solution)/shard_map/cond
  391.8 11.9 %copy-start.47 = (bf16[256,768]{1,0:T(8,128)(2,1)S(1)}, bf16[256,768]{1,0:T(8,128)(2,1)}, u32[]{:S(2)}) copy-start(bf16[256,768]{1,0:T(8,128)(2,1)} %get-tuple-element.139) | copy-start | bytes 1179652 | tf_op jit(solution)/shard_map/cond
  414.9 170.3 %copy-start.66 = (f32[16,768]{1,0:T(8,128)S(1)}, f32[16,768]{1,0:T(8,128)}, u32[]{:S(2)}) copy-start(f32[16,768]{1,0:T(8,128)} %get-tuple-element.311) | copy-start | bytes 147460
  585.2 9.2 %copy-start.35 = (bf16[256,768]{1,0:T(8,128)(2,1)S(1)}, bf16[256,768]{1,0:T(8,128)(2,1)}, u32[]{:S(2)}) copy-start(bf16[256,768]{1,0:T(8,128)(2,1)} %copy-done.34) | copy-start | bytes 1179652
  585.2 9.2 %copy-start.38 = (bf16[1,1,256,768]{3,2,1,0:T(8,128)(2,1)S(1)}, bf16[1,1,256,768]{3,2,1,0:T(8,128)(2,1)}, u32[]{:S(2)}) copy-start(bf16[1,1,256,768]{3,2,1,0:T(8,128)(2,1)} %fusion.196) | copy-start | bytes 1179652
  585.2 9.2 %copy-start.40 = (bf16[256,768]{1,0:T(8,128)(2,1)S(1)}, bf16[256,768]{1,0:T(8,128)(2,1)}, u32[]{:S(2)}) copy-start(bf16[256,768]{1,0:T(8,128)(2,1)} %copy-done.39) | copy-start | bytes 1179652
  594.2 7.1 %copy-start.17 = (f32[1,3072,768]{2,1,0:T(8,128)}, f32[1,3072,768]{2,1,0:T(8,128)S(1)}, u32[]{:S(2)}) copy-start(f32[1,3072,768]{2,1,0:T(8,128)S(1)} %get-tuple-element.411) | copy-start | bytes 28311556
  594.2 7.6 %copy-start.27 = (f32[1,768,768]{2,1,0:T(8,128)}, f32[1,768,768]{2,1,0:T(8,128)S(1)}, u32[]{:S(2)}) copy-start(f32[1,768,768]{2,1,0:T(8,128)S(1)} %get-tuple-element.409) | copy-start | bytes 7077892
  594.2 7.6 %copy-start.82 = (f32[1,5,768]{2,0,1:T(1,128)}, f32[1,5,768]{2,0,1:T(1,128)S(1)}, u32[]{:S(2)}) copy-start(f32[1,5,768]{2,0,1:T(1,128)S(1)} %get-tuple-element.418) | copy-start | bytes 46084
  594.3 7.5 %copy-start.83 = (f32[1,5,768]{2,0,1:T(1,128)}, f32[1,5,768]{2,0,1:T(1,128)S(1)}, u32[]{:S(2)}) copy-start(f32[1,5,768]{2,0,1:T(1,128)S(1)} %get-tuple-element.419) | copy-start | bytes 46084
  594.3 7.5 %copy-start.90 = (f32[1,768]{1,0:T(1,128)}, f32[1,768]{1,0:T(1,128)S(1)}, u32[]{:S(2)}) copy-start(f32[1,768]{1,0:T(1,128)S(1)} %get-tuple-element.417) | copy-start | bytes 9220
  594.3 7.5 %copy-start.91 = (f32[1,768]{1,0:T(1,128)}, f32[1,768]{1,0:T(1,128)S(1)}, u32[]{:S(2)}) copy-start(f32[1,768]{1,0:T(1,128)S(1)} %get-tuple-element.416) | copy-start | bytes 9220
  594.3 7.5 %copy-start.92 = (f32[1,768]{1,0:T(1,128)}, f32[1,768]{1,0:T(1,128)S(1)}, u32[]{:S(2)}) copy-start(f32[1,768]{1,0:T(1,128)S(1)} %get-tuple-element.415) | copy-start | bytes 9220
  594.3 7.5 %copy-start.93 = (f32[1,768]{1,0:T(1,128)}, f32[1,768]{1,0:T(1,128)S(1)}, u32[]{:S(2)}) copy-start(f32[1,768]{1,0:T(1,128)S(1)} %get-tuple-element.414) | copy-start | bytes 9220
  (60 other events, 179.1 us)
